TPU v7x, 512 devices: a whole 4x4x16 slice. The times are simulated.
512 devices in a mesh: blk: 16 (over x_lo, y, core), group: 32 (over x_hi, z).
Axes of the slice: x: 4 (x_hi: 2, x_lo: 2; x = x_hi * 2 + x_lo), y: 4, z: 16, core: 2. Of those that a mesh axis runs over, the one named last changes fastest.
Arguments:
- queries: bfloat16 [512, 16, 128], P(('blk', 'group')), may hold values from -2.5 to 2.5
- query_mask: int32 [512, 16], P(('blk', 'group')), may hold values from 0 to 1, as said below
- positive: int32 [512], P(('blk', 'group')), may hold values from 0 to 1023
- page_vectors: bfloat16 [1024, 128, 128], P(('blk', 'group')), may hold values from -2 to 2
- page_mask: int32 [1024, 128], P(('blk', 'group')), may hold values from 0 to 1, as said below
Outputs:
- grad_queries: float32 [512, 16, 128], P(('blk', 'group'))
- grad_pages: float32 [1024, 128, 128], P(('blk', 'group'))
- mean_loss: float32 [], replicated
Inputs may be any that keep to these rules, and one draw needn't show every extreme that they name: `query_mask`: each row holds ones on its first 8 to 16 token slots and zeros after them. `page_mask`: each row holds ones on its first 32 to 128 patch slots and zeros after them.
All inputs are finite; a program needn't handle non-finite values.
Results may differ from a plain program's by a relative error of at most 0.0028.
Values may be sent and summed in bfloat16 or wider, within the bound.
A program may use at most 64 MiB of HBM per device.

v0:
```python
import functools
import math

import jax
import jax.numpy as jnp
from jax import lax
from jax.sharding import Mesh
from jax.sharding import PartitionSpec as P

BLK = ("blk_0", "blk_1", "blk_2")
GROUP = ("group_0", "group_1")
BLK_GROUP = ("blk_0", "blk_1", "blk_2", "group_0", "group_1")


relaxation_scale_factor = 0.5
guarded_floor_entry = -1e30


def side_by_side(arrays, axis, dim, along):
    columns = [a.reshape(*a.shape[:along], -1) for a in arrays]
    both = jnp.concatenate(columns, axis=along)
    result, at, gathered = (lax.all_gather(both, axis, axis=dim, tiled=True), 0, [])
    for a, column in zip(arrays, columns):
        section = result[..., at : at + column.shape[along]]
        gathered.append(section.reshape(*section.shape[:along], *a.shape[along:]))
        at += column.shape[along]
    return tuple(gathered)


def over_axes(x, axes):
    return functools.reduce(lax.pmax, axes, x)


def one_axis_at_a_time(x, axes):
    for axis in axes:
        x = lax.psum(x, axis)
    return x


def from_behind(value, axis, steps):
    count = lax.axis_size(axis)
    pairs = [(source, (source + steps) % count) for source in range(count)]
    return lax.ppermute(value, axis, pairs)


def cut_along(x, dim, size):
    before, after = (x.shape[:dim], x.shape[dim + 1 :])
    return jnp.moveaxis(x.reshape(*before, size, -1, *after), dim, 0)


def sum_at_owner(x, axis, dim):
    size = lax.axis_size(axis)
    pieces = lax.all_to_all(cut_along(x, dim, size), axis, 0, 0, tiled=True)
    return jnp.sum(pieces, axis=0)


def masked_logits(row_block, lone_document, live_image_embeddings):
    similarity_matrix = lax.dot_general(
        row_block, lone_document, (((1,), (1,)), ((), ())), preferred_element_type=jnp.float32
    )
    return jnp.where(
        live_image_embeddings[None, :] > 0,
        similarity_matrix / relaxation_scale_factor,
        guarded_floor_entry,
    )


def on_device(queries, query_mask, positive, page_vectors, page_mask):
    tokens = queries.shape[1]
    features = queries.shape[2]
    local_pages = page_vectors.shape[0]
    blocks = lax.axis_size(BLK)
    members = lax.axis_size(GROUP)
    bundle_size = queries.shape[0] * members
    total_queries = bundle_size * blocks
    natural_logarithm_lengths = jnp.log(jnp.sum(page_mask.astype(jnp.float32), axis=1))
    bundle_vectors, bundle_masks, bundle_targets = (
        lax.all_gather(queries, GROUP, axis=0, tiled=True),
        *side_by_side((query_mask, positive), GROUP, 0, 1),
    )

    def forward_piece(folded, shard_in, root_row):
        scores, lse_rows, live_all, owners, kept = folded
        vectors, token_masks, targets = shard_in
        amount = vectors.shape[0]
        stride = math.gcd(amount, max(1, 512 // tokens))

        def run_block(number, current):
            scores, lse_rows = current
            offset = number * stride
            slab_rows = lax.dynamic_slice_in_dim(vectors, offset, stride, 0).reshape(
                stride * tokens, features
            )
            alive = lax.dynamic_slice_in_dim(token_masks, offset, stride, 0).astype(jnp.float32)
            found_sums = []
            for index_page in range(local_pages):
                masked = masked_logits(slab_rows, page_vectors[index_page], page_mask[index_page])
                highest = jnp.max(masked, axis=1, keepdims=True)
                found_sums.append(
                    highest[:, 0] + jnp.log(jnp.sum(jnp.exp(masked - highest), axis=1))
                )
            logsumexp_results = jnp.stack(found_sums, axis=1).reshape(stride, tokens, local_pages)
            softened_supremum = relaxation_scale_factor * (
                logsumexp_results - natural_logarithm_lengths
            )
            page_score = jnp.sum(alive[:, :, None] * softened_supremum, axis=1)
            scores = lax.dynamic_update_slice_in_dim(scores, page_score, offset, 0)
            lse_rows = lax.dynamic_update_slice_in_dim(lse_rows, logsumexp_results, offset, 0)
            return (scores, lse_rows)

        scores, lse_rows = lax.fori_loop(0, amount // stride, run_block, (scores, lse_rows))
        live_all = lax.dynamic_update_slice_in_dim(live_all, token_masks, root_row, 0)
        owners = lax.dynamic_update_slice_in_dim(owners, targets, root_row, 0)
        kept = vectors
        return (scores, lse_rows, live_all, owners, kept)

    starting = (
        jnp.zeros((total_queries, local_pages), jnp.float32),
        jnp.zeros((total_queries, tokens, local_pages), jnp.float32),
        jnp.zeros((total_queries, tokens), jnp.int32),
        jnp.zeros((total_queries,), jnp.int32),
        jnp.zeros((total_queries, tokens, features), jnp.bfloat16),
    )
    scores, lse_rows, live_all, owners, kept = forward_piece(
        starting,
        (
            lax.all_gather(bundle_vectors, BLK, axis=0, tiled=True),
            lax.all_gather(bundle_masks, BLK, axis=0, tiled=True),
            lax.all_gather(bundle_targets, BLK, axis=0, tiled=True),
        ),
        jnp.int32(0),
    )
    position = lax.axis_index(BLK_GROUP)
    page_ids = position * local_pages + jnp.arange(local_pages, dtype=jnp.int32)
    chosen = owners[:, None] == page_ids[None, :]
    picked_local = jnp.sum(jnp.where(chosen, scores, 0.0))
    local_top = jnp.max(scores, axis=1)
    highest = over_axes(local_top, BLK_GROUP)
    local_total = jnp.sum(jnp.exp(scores - highest[:, None]), axis=1)
    totals, picked = (
        one_axis_at_a_time(local_total, BLK_GROUP),
        one_axis_at_a_time(picked_local, BLK_GROUP),
    )
    page_lse = highest + jnp.log(totals)
    mean_loss = (jnp.sum(page_lse) - picked) / total_queries
    coefficient = jnp.exp(scores - page_lse[:, None]) - chosen.astype(jnp.float32)
    factor_scale = coefficient[:, None, :] * live_all.astype(jnp.float32)[:, :, None]

    def slice_rows(root_row, amount):
        sums = lax.dynamic_slice_in_dim(lse_rows, root_row, amount, 0).reshape(
            amount * tokens, local_pages
        )
        scales = lax.dynamic_slice_in_dim(factor_scale, root_row, amount, 0).reshape(
            amount * tokens, local_pages
        )
        return (sums, scales)

    def gradient_terms(row_block, logsumexp_results, scales, page_grads):
        partial_value = jnp.zeros(row_block.shape, jnp.float32)
        for number in range(local_pages):
            masked = masked_logits(row_block, page_vectors[number], page_mask[number])
            weights = jnp.exp(masked - logsumexp_results[:, number : number + 1])
            factor = (scales[:, number : number + 1] * weights).astype(jnp.bfloat16)
            partial_value = partial_value + jnp.dot(
                factor, page_vectors[number], preferred_element_type=jnp.float32
            )
            update = lax.dot_general(
                factor, row_block, (((0,), (0,)), ((), ())), preferred_element_type=jnp.float32
            )
            page_grads = page_grads.at[number].add(update)
        return (partial_value, page_grads)

    home = lax.axis_index(BLK)
    page_grads = jnp.zeros(page_vectors.shape, jnp.float32)

    def visit_one(moving, collected, page_grads, lap_index):
        root_row = (home - lap_index) % blocks * bundle_size
        sums, scales = slice_rows(root_row, bundle_size)
        partial_value, page_grads = gradient_terms(
            moving.reshape(bundle_size * tokens, features), sums, scales, page_grads
        )
        return (collected + partial_value.reshape(bundle_size, tokens, features), page_grads)

    def pass_one(collected):
        return from_behind(collected, BLK, 1)

    def turn_one(lap_index, current):
        moving, collected, page_grads = current
        collected, page_grads = visit_one(moving, collected, page_grads, lap_index)
        moving = from_behind(moving, BLK, 1)
        return (moving, pass_one(collected), page_grads)

    empty_whole = jnp.zeros((bundle_size, tokens, features), jnp.float32)
    moving, collected, page_grads = lax.fori_loop(
        0, blocks - 1, turn_one, (bundle_vectors, empty_whole, page_grads)
    )
    collected, page_grads = visit_one(moving, collected, page_grads, blocks - 1)
    collected = pass_one(collected)
    grad_queries = sum_at_owner(collected, GROUP, 0)
    return (grad_queries, page_grads, mean_loss)


def solution(mesh):
    split = Mesh(
        mesh.devices.reshape(2, 4, 2, 2, 16), ("blk_0", "blk_1", "blk_2", "group_0", "group_1")
    )
    return jax.shard_map(
        on_device,
        mesh=split,
        in_specs=(
            P(BLK_GROUP, None, None),
            P(BLK_GROUP, None),
            P(BLK_GROUP),
            P(BLK_GROUP, None, None),
            P(BLK_GROUP, None),
        ),
        out_specs=(P(BLK_GROUP, None, None), P(BLK_GROUP, None, None), P()),
        check_vma=False,
    )
```

profile of v0, /device:TPU:2, one launch (start us, length us, event | category | flops | bytes accessed | tf_op | source)
XLA Modules:
  0.0 667.9 jit_solution(16827437556974625158)
XLA Ops:
  7.2 87.3 %all_gather.15 = bf16[32,16,128]{2,1,0:T(8,128)(2,1)} all-gather(bf16[1,16,128]{2,1,0:T(8,128)(2,1)} %param.17), channel_id=1, replica_groups=mesh['blk_0'=2,'blk_1'=4,'blk_2'=2,'group_0'=2,'group_1'=16] {'group_0',..., dimensions={0}, use_global_device_ids=true | all-gather | bytes 135168 | tf_op jit(solution)/shard_map/all_gather | solution.py:78
  95.9 70.5 %all-gather.1 = s32[32,1,17]{2,1,0:T(1,128)S(1)} all-gather(s32[1,1,17]{2,1,0:T(1,128)S(1)} %add_bitcast_fusion), channel_id=1, replica_groups=mesh['blk_0'=2,'blk_1'=4,'blk_2'=2,'group_0'=2,'group_1'=16] {'group_0',..., dimensions={0}, use_global_device_ids=true | all-gather | bytes 2244 | tf_op jit(solution)/shard_map/all_gather | solution.py:22
  166.4 20.1 %all-gather.2 = s32[16,32,16]{1,2,0:T(8,128)S(1)} all-gather(s32[1,32,16]{1,2,0:T(8,128)S(1)} %copy.11), channel_id=1, replica_groups=mesh['blk_0'=2,'blk_1'=4,'blk_2'=2,'group_0'=2,'group_1'=16] {'blk_0','b..., dimensions={0}, use_global_device_ids=true | all-gather | bytes 34816 | tf_op jit(solution)/shard_map/all_gather | solution.py:128
  190.0 8.0 %all-reduce = s32[512]{0:T(512)S(1)} all-reduce(s32[512]{0:T(512)S(1)} %dynamic-update-slice.26), channel_id=2, replica_groups=mesh['blk_0'=2,'blk_1'=4,'blk_2'=2,'group_0'=2,'group_1'=16] {'blk_0','b..., use_global_device_ids=true, to_apply=%add | all-reduce | flops 512 | bytes 4096
  198.9 72.4 %while.38 = (s32[]{:T(128)}, f32[512,2]{0,1:T(2,128)S(1)}, f32[512,16,2]{1,0,2:T(8,128)S(1)}, s32[2,128]{1,0:T(2,128)}, bf16[512,16,128]{2,1,0:T(8,128)(2,1)}, /...) while((s32[]{:T(128)}, f32[512,2]{0,1:T(2,128)S(1)}, ...), condition=%wide.region_7.8_spmd, body=%wide.region_1.7_spmd.sunk | while | flops 34213060 | bytes 1820339 | solution.py:111
  271.3 4.9 pmax.35
  276.2 11.6 %pmax.36 = f32[512]{0:T(512)S(1)} all-reduce(f32[512]{0:T(512)S(1)} %pmax.35), channel_id=1, replica_groups=mesh['blk_0'=2,'blk_1'=4,'blk_2'=2,'group_0'=2,'group_1'=16] {'blk_1'}, use_global_device_ids=true, to_apply=%region_10.11 | all-reduce | flops 512 | bytes 4096 | tf_op jit(solution)/shard_map/pmax | solution.py:31
  290.2 6.4 pmax.38
  296.7 29.0 %pmax.39 = f32[512]{0:T(512)S(1)} all-reduce(f32[512]{0:T(512)S(1)} %pmax.38), channel_id=1, replica_groups=mesh['blk_0'=2,'blk_1'=4,'blk_2'=2,'group_0'=2,'group_1'=16] {'group_1'}, use_global_device_ids=true, to_apply=%region_13.14 | all-reduce | flops 512 | bytes 4096 | tf_op jit(solution)/shard_map/pmax | solution.py:31
  326.4 5.5 all-reduce.5
  331.9 8.3 %all-reduce.2 = (f32[512]{0:T(512)S(1)}, f32[]{:T(128)}) all-reduce(f32[512]{0:T(512)S(1)} %get-tuple-element.502, f32[]{:T(128)} %get-tuple-element.503), channel_id=1, replica_groups=mesh['blk_0'=2,'blk_1'=4,'blk_2'=2,'group_0'=2,'group_1'=16] {'blk_1'}, use_global_device_ids=true, to_apply=%region_16.17 | all-reduce | flops 513 | bytes 4104 | tf_op jit(solution)/shard_map/psum | solution.py:36
  343.3 7.0 %all-reduce.3 = (f32[512]{0:T(512)S(1)}, f32[]{:T(128)}) all-reduce(f32[512]{0:T(512)S(1)} %get-tuple-element.500, f32[]{:T(128)} %get-tuple-element.501), channel_id=1, replica_groups=mesh['blk_0'=2,'blk_1'=4,'blk_2'=2,'group_0'=2,'group_1'=16] {'group_0'}, use_global_device_ids=true, to_apply=%region_18.19 | all-reduce | flops 513 | bytes 4104 | tf_op jit(solution)/shard_map/psum | solution.py:36
  350.4 27.6 %all-reduce.1 = (f32[512]{0:T(512)S(1)}, f32[]{:T(128)}) all-reduce(f32[512]{0:T(512)S(1)} %get-tuple-element.498, f32[]{:T(128)} %get-tuple-element.499), channel_id=1, replica_groups=mesh['blk_0'=2,'blk_1'=4,'blk_2'=2,'group_0'=2,'group_1'=16] {'group_1'}, use_global_device_ids=true, to_apply=%region_19.20 | all-reduce | flops 513 | bytes 4104 | tf_op jit(solution)/shard_map/psum | solution.py:36
  379.3 240.3 %while.39 = (s32[]{:T(128)}, bf16[32,16,128]{2,1,0:T(8,128)(2,1)S(1)}, f32[32,16,128]{2,1,0:T(8,128)S(1)}, f32[2,128,128]{2,1,0:T(8,128)S(1)}, s32[]{:T(128)}, /...) while((s32[]{:T(128)}, ...), condition=%wide.region_21.22_spmd, body=%wide.region_20.21_spmd.sunk | while | flops 101482768 | bytes 5433252 | solution.py:194
  389.9 5.3 collective-permute-done.1
  403.8 7.4 %collective-permute-done.1 = f32[32,16,128]{2,1,0:T(8,128)S(1)} collective-permute-done((f32[32,16,128]{2,1,0:T(8,128)S(1)}, f32[32,16,128]{2,1,0:T(8,128)S(1)}, u32[]{:S(2)}, u32[]{:S(2)}) %collective-permute-start.1) | collective-permute-done | bytes 262176 | tf_op jit(solution)/shard_map/while/body/eval_jaxpr/ppermute | solution.py:43
  419.8 7.4 %collective-permute-done.1 = f32[32,16,128]{2,1,0:T(8,128)S(1)} collective-permute-done((f32[32,16,128]{2,1,0:T(8,128)S(1)}, f32[32,16,128]{2,1,0:T(8,128)S(1)}, u32[]{:S(2)}, u32[]{:S(2)}) %collective-permute-start.1) | collective-permute-done | bytes 262176 | tf_op jit(solution)/shard_map/while/body/eval_jaxpr/ppermute | solution.py:43
  435.9 7.4 %collective-permute-done.1 = f32[32,16,128]{2,1,0:T(8,128)S(1)} collective-permute-done((f32[32,16,128]{2,1,0:T(8,128)S(1)}, f32[32,16,128]{2,1,0:T(8,128)S(1)}, u32[]{:S(2)}, u32[]{:S(2)}) %collective-permute-start.1) | collective-permute-done | bytes 262176 | tf_op jit(solution)/shard_map/while/body/eval_jaxpr/ppermute | solution.py:43
  451.9 7.4 %collective-permute-done.1 = f32[32,16,128]{2,1,0:T(8,128)S(1)} collective-permute-done((f32[32,16,128]{2,1,0:T(8,128)S(1)}, f32[32,16,128]{2,1,0:T(8,128)S(1)}, u32[]{:S(2)}, u32[]{:S(2)}) %collective-permute-start.1) | collective-permute-done | bytes 262176 | tf_op jit(solution)/shard_map/while/body/eval_jaxpr/ppermute | solution.py:43
  467.9 7.4 %collective-permute-done.1 = f32[32,16,128]{2,1,0:T(8,128)S(1)} collective-permute-done((f32[32,16,128]{2,1,0:T(8,128)S(1)}, f32[32,16,128]{2,1,0:T(8,128)S(1)}, u32[]{:S(2)}, u32[]{:S(2)}) %collective-permute-start.1) | collective-permute-done | bytes 262176 | tf_op jit(solution)/shard_map/while/body/eval_jaxpr/ppermute | solution.py:43
  483.9 7.4 %collective-permute-done.1 = f32[32,16,128]{2,1,0:T(8,128)S(1)} collective-permute-done((f32[32,16,128]{2,1,0:T(8,128)S(1)}, f32[32,16,128]{2,1,0:T(8,128)S(1)}, u32[]{:S(2)}, u32[]{:S(2)}) %collective-permute-start.1) | collective-permute-done | bytes 262176 | tf_op jit(solution)/shard_map/while/body/eval_jaxpr/ppermute | solution.py:43
  500.0 7.4 %collective-permute-done.1 = f32[32,16,128]{2,1,0:T(8,128)S(1)} collective-permute-done((f32[32,16,128]{2,1,0:T(8,128)S(1)}, f32[32,16,128]{2,1,0:T(8,128)S(1)}, u32[]{:S(2)}, u32[]{:S(2)}) %collective-permute-start.1) | collective-permute-done | bytes 262176 | tf_op jit(solution)/shard_map/while/body/eval_jaxpr/ppermute | solution.py:43
  516.0 7.4 %collective-permute-done.1 = f32[32,16,128]{2,1,0:T(8,128)S(1)} collective-permute-done((f32[32,16,128]{2,1,0:T(8,128)S(1)}, f32[32,16,128]{2,1,0:T(8,128)S(1)}, u32[]{:S(2)}, u32[]{:S(2)}) %collective-permute-start.1) | collective-permute-done | bytes 262176 | tf_op jit(solution)/shard_map/while/body/eval_jaxpr/ppermute | solution.py:43
  532.0 7.4 %collective-permute-done.1 = f32[32,16,128]{2,1,0:T(8,128)S(1)} collective-permute-done((f32[32,16,128]{2,1,0:T(8,128)S(1)}, f32[32,16,128]{2,1,0:T(8,128)S(1)}, u32[]{:S(2)}, u32[]{:S(2)}) %collective-permute-start.1) | collective-permute-done | bytes 262176 | tf_op jit(solution)/shard_map/while/body/eval_jaxpr/ppermute | solution.py:43
  548.0 7.4 %collective-permute-done.1 = f32[32,16,128]{2,1,0:T(8,128)S(1)} collective-permute-done((f32[32,16,128]{2,1,0:T(8,128)S(1)}, f32[32,16,128]{2,1,0:T(8,128)S(1)}, u32[]{:S(2)}, u32[]{:S(2)}) %collective-permute-start.1) | collective-permute-done | bytes 262176 | tf_op jit(solution)/shard_map/while/body/eval_jaxpr/ppermute | solution.py:43
  564.1 7.4 %collective-permute-done.1 = f32[32,16,128]{2,1,0:T(8,128)S(1)} collective-permute-done((f32[32,16,128]{2,1,0:T(8,128)S(1)}, f32[32,16,128]{2,1,0:T(8,128)S(1)}, u32[]{:S(2)}, u32[]{:S(2)}) %collective-permute-start.1) | collective-permute-done | bytes 262176 | tf_op jit(solution)/shard_map/while/body/eval_jaxpr/ppermute | solution.py:43
  580.1 7.4 %collective-permute-done.1 = f32[32,16,128]{2,1,0:T(8,128)S(1)} collective-permute-done((f32[32,16,128]{2,1,0:T(8,128)S(1)}, f32[32,16,128]{2,1,0:T(8,128)S(1)}, u32[]{:S(2)}, u32[]{:S(2)}) %collective-permute-start.1) | collective-permute-done | bytes 262176 | tf_op jit(solution)/shard_map/while/body/eval_jaxpr/ppermute | solution.py:43
  596.1 7.4 %collective-permute-done.1 = f32[32,16,128]{2,1,0:T(8,128)S(1)} collective-permute-done((f32[32,16,128]{2,1,0:T(8,128)S(1)}, f32[32,16,128]{2,1,0:T(8,128)S(1)}, u32[]{:S(2)}, u32[]{:S(2)}) %collective-permute-start.1) | collective-permute-done | bytes 262176 | tf_op jit(solution)/shard_map/while/body/eval_jaxpr/ppermute | solution.py:43
  612.1 7.4 %collective-permute-done.1 = f32[32,16,128]{2,1,0:T(8,128)S(1)} collective-permute-done((f32[32,16,128]{2,1,0:T(8,128)S(1)}, f32[32,16,128]{2,1,0:T(8,128)S(1)}, u32[]{:S(2)}, u32[]{:S(2)}) %collective-permute-start.1) | collective-permute-done | bytes 262176 | tf_op jit(solution)/shard_map/while/body/eval_jaxpr/ppermute | solution.py:43
  625.4 8.0 %collective-permute-done.2 = f32[32,16,128]{2,1,0:T(8,128)} collective-permute-done((f32[32,16,128]{2,1,0:T(8,128)S(1)}, f32[32,16,128]{2,1,0:T(8,128)}, u32[]{:S(2)}, u32[]{:S(2)}) %collective-permute-start.2) | collective-permute-done | bytes 262176 | tf_op jit(solution)/shard_map/ppermute | solution.py:43
  633.3 6.3 all-to-all-start
  641.4 17.8 %all-to-all-done = f32[32,1,16,128]{3,2,1,0:T(8,128)S(1)} async-done(((f32[32,1,16,128]{3,2,1,0:T(8,128)}), f32[32,1,16,128]{3,2,1,0:T(8,128)S(1)}, u32[]{:S(2)}, u32[]{:S(2)}) %all-to-all-start) | async-done | bytes 262176 | tf_op jit(solution)/shard_map/all_to_all | solution.py:53
  (605 shorter events, 220.3 us)
Async XLA Ops:
  7.2 191.7 %all-gather.5.cloned.1.call-start = ((), (), s32[]{:S(2)}) async-start(), calls=%async_computation.1 | async-start | bytes 2228224 | tf_op jit(solution)/shard_map/all_gather | solution.py:127
  379.3 10.6 %collective-permute-start = (bf16[32,16,128]{2,1,0:T(8,128)(2,1)S(1)}, bf16[32,16,128]{2,1,0:T(8,128)(2,1)S(1)}, u32[]{:S(2)}, u32[]{:S(2)}) collective-permute-start(bf16[32,16,128]{2,1,0:T(8,128)(2,1)S(1)} %copy.38), channel_id=1, source_target_pairs={{0,32},{32,64},{64,96},{96,128},{128,160},{160,192},{192,224},{224... | collective-permute-start | bytes 393224 | tf_op jit(solution)/shard_map/while/body/eval_jaxpr/ppermute | solution.py:43
  385.4 9.8 %collective-permute-start.1 = (f32[32,16,128]{2,1,0:T(8,128)S(1)}, f32[32,16,128]{2,1,0:T(8,128)S(1)}, u32[]{:S(2)}, u32[]{:S(2)}) collective-permute-start(f32[32,16,128]{2,1,0:T(8,128)S(1)} %add.300), channel_id=1, source_target_pairs={{0,32},{32,64},{64,96},{96,128},{128,160},{160,192},{192,224},{224... | collective-permute-start | bytes 786440 | tf_op jit(solution)/shard_map/while/body/eval_jaxpr/ppermute | solution.py:43
  395.2 8.6 %collective-permute-start = (bf16[32,16,128]{2,1,0:T(8,128)(2,1)S(1)}, bf16[32,16,128]{2,1,0:T(8,128)(2,1)S(1)}, u32[]{:S(2)}, u32[]{:S(2)}) collective-permute-start(bf16[32,16,128]{2,1,0:T(8,128)(2,1)S(1)} %copy.38), channel_id=1, source_target_pairs={{0,32},{32,64},{64,96},{96,128},{128,160},{160,192},{192,224},{224... | collective-permute-start | bytes 393224 | tf_op jit(solution)/shard_map/while/body/eval_jaxpr/ppermute | solution.py:43
  401.4 9.8 %collective-permute-start.1 = (f32[32,16,128]{2,1,0:T(8,128)S(1)}, f32[32,16,128]{2,1,0:T(8,128)S(1)}, u32[]{:S(2)}, u32[]{:S(2)}) collective-permute-start(f32[32,16,128]{2,1,0:T(8,128)S(1)} %add.300), channel_id=1, source_target_pairs={{0,32},{32,64},{64,96},{96,128},{128,160},{160,192},{192,224},{224... | collective-permute-start | bytes 786440 | tf_op jit(solution)/shard_map/while/body/eval_jaxpr/ppermute | solution.py:43
  411.2 8.6 %collective-permute-start = (bf16[32,16,128]{2,1,0:T(8,128)(2,1)S(1)}, bf16[32,16,128]{2,1,0:T(8,128)(2,1)S(1)}, u32[]{:S(2)}, u32[]{:S(2)}) collective-permute-start(bf16[32,16,128]{2,1,0:T(8,128)(2,1)S(1)} %copy.38), channel_id=1, source_target_pairs={{0,32},{32,64},{64,96},{96,128},{128,160},{160,192},{192,224},{224... | collective-permute-start | bytes 393224 | tf_op jit(solution)/shard_map/while/body/eval_jaxpr/ppermute | solution.py:43
  417.4 9.8 %collective-permute-start.1 = (f32[32,16,128]{2,1,0:T(8,128)S(1)}, f32[32,16,128]{2,1,0:T(8,128)S(1)}, u32[]{:S(2)}, u32[]{:S(2)}) collective-permute-start(f32[32,16,128]{2,1,0:T(8,128)S(1)} %add.300), channel_id=1, source_target_pairs={{0,32},{32,64},{64,96},{96,128},{128,160},{160,192},{192,224},{224... | collective-permute-start | bytes 786440 | tf_op jit(solution)/shard_map/while/body/eval_jaxpr/ppermute | solution.py:43
  427.2 8.6 %collective-permute-start = (bf16[32,16,128]{2,1,0:T(8,128)(2,1)S(1)}, bf16[32,16,128]{2,1,0:T(8,128)(2,1)S(1)}, u32[]{:S(2)}, u32[]{:S(2)}) collective-permute-start(bf16[32,16,128]{2,1,0:T(8,128)(2,1)S(1)} %copy.38), channel_id=1, source_target_pairs={{0,32},{32,64},{64,96},{96,128},{128,160},{160,192},{192,224},{224... | collective-permute-start | bytes 393224 | tf_op jit(solution)/shard_map/while/body/eval_jaxpr/ppermute | solution.py:43
  433.5 9.8 %collective-permute-start.1 = (f32[32,16,128]{2,1,0:T(8,128)S(1)}, f32[32,16,128]{2,1,0:T(8,128)S(1)}, u32[]{:S(2)}, u32[]{:S(2)}) collective-permute-start(f32[32,16,128]{2,1,0:T(8,128)S(1)} %add.300), channel_id=1, source_target_pairs={{0,32},{32,64},{64,96},{96,128},{128,160},{160,192},{192,224},{224... | collective-permute-start | bytes 786440 | tf_op jit(solution)/shard_map/while/body/eval_jaxpr/ppermute | solution.py:43
  443.3 8.6 %collective-permute-start = (bf16[32,16,128]{2,1,0:T(8,128)(2,1)S(1)}, bf16[32,16,128]{2,1,0:T(8,128)(2,1)S(1)}, u32[]{:S(2)}, u32[]{:S(2)}) collective-permute-start(bf16[32,16,128]{2,1,0:T(8,128)(2,1)S(1)} %copy.38), channel_id=1, source_target_pairs={{0,32},{32,64},{64,96},{96,128},{128,160},{160,192},{192,224},{224... | collective-permute-start | bytes 393224 | tf_op jit(solution)/shard_map/while/body/eval_jaxpr/ppermute | solution.py:43
  449.5 9.8 %collective-permute-start.1 = (f32[32,16,128]{2,1,0:T(8,128)S(1)}, f32[32,16,128]{2,1,0:T(8,128)S(1)}, u32[]{:S(2)}, u32[]{:S(2)}) collective-permute-start(f32[32,16,128]{2,1,0:T(8,128)S(1)} %add.300), channel_id=1, source_target_pairs={{0,32},{32,64},{64,96},{96,128},{128,160},{160,192},{192,224},{224... | collective-permute-start | bytes 786440 | tf_op jit(solution)/shard_map/while/body/eval_jaxpr/ppermute | solution.py:43
  459.3 8.6 %collective-permute-start = (bf16[32,16,128]{2,1,0:T(8,128)(2,1)S(1)}, bf16[32,16,128]{2,1,0:T(8,128)(2,1)S(1)}, u32[]{:S(2)}, u32[]{:S(2)}) collective-permute-start(bf16[32,16,128]{2,1,0:T(8,128)(2,1)S(1)} %copy.38), channel_id=1, source_target_pairs={{0,32},{32,64},{64,96},{96,128},{128,160},{160,192},{192,224},{224... | collective-permute-start | bytes 393224 | tf_op jit(solution)/shard_map/while/body/eval_jaxpr/ppermute | solution.py:43
  465.5 9.8 %collective-permute-start.1 = (f32[32,16,128]{2,1,0:T(8,128)S(1)}, f32[32,16,128]{2,1,0:T(8,128)S(1)}, u32[]{:S(2)}, u32[]{:S(2)}) collective-permute-start(f32[32,16,128]{2,1,0:T(8,128)S(1)} %add.300), channel_id=1, source_target_pairs={{0,32},{32,64},{64,96},{96,128},{128,160},{160,192},{192,224},{224... | collective-permute-start | bytes 786440 | tf_op jit(solution)/shard_map/while/body/eval_jaxpr/ppermute | solution.py:43
  475.3 8.6 %collective-permute-start = (bf16[32,16,128]{2,1,0:T(8,128)(2,1)S(1)}, bf16[32,16,128]{2,1,0:T(8,128)(2,1)S(1)}, u32[]{:S(2)}, u32[]{:S(2)}) collective-permute-start(bf16[32,16,128]{2,1,0:T(8,128)(2,1)S(1)} %copy.38), channel_id=1, source_target_pairs={{0,32},{32,64},{64,96},{96,128},{128,160},{160,192},{192,224},{224... | collective-permute-start | bytes 393224 | tf_op jit(solution)/shard_map/while/body/eval_jaxpr/ppermute | solution.py:43
  481.5 9.8 %collective-permute-start.1 = (f32[32,16,128]{2,1,0:T(8,128)S(1)}, f32[32,16,128]{2,1,0:T(8,128)S(1)}, u32[]{:S(2)}, u32[]{:S(2)}) collective-permute-start(f32[32,16,128]{2,1,0:T(8,128)S(1)} %add.300), channel_id=1, source_target_pairs={{0,32},{32,64},{64,96},{96,128},{128,160},{160,192},{192,224},{224... | collective-permute-start | bytes 786440 | tf_op jit(solution)/shard_map/while/body/eval_jaxpr/ppermute | solution.py:43
  491.3 8.6 %collective-permute-start = (bf16[32,16,128]{2,1,0:T(8,128)(2,1)S(1)}, bf16[32,16,128]{2,1,0:T(8,128)(2,1)S(1)}, u32[]{:S(2)}, u32[]{:S(2)}) collective-permute-start(bf16[32,16,128]{2,1,0:T(8,128)(2,1)S(1)} %copy.38), channel_id=1, source_target_pairs={{0,32},{32,64},{64,96},{96,128},{128,160},{160,192},{192,224},{224... | collective-permute-start | bytes 393224 | tf_op jit(solution)/shard_map/while/body/eval_jaxpr/ppermute | solution.py:43
  497.6 9.8 %collective-permute-start.1 = (f32[32,16,128]{2,1,0:T(8,128)S(1)}, f32[32,16,128]{2,1,0:T(8,128)S(1)}, u32[]{:S(2)}, u32[]{:S(2)}) collective-permute-start(f32[32,16,128]{2,1,0:T(8,128)S(1)} %add.300), channel_id=1, source_target_pairs={{0,32},{32,64},{64,96},{96,128},{128,160},{160,192},{192,224},{224... | collective-permute-start | bytes 786440 | tf_op jit(solution)/shard_map/while/body/eval_jaxpr/ppermute | solution.py:43
  507.4 8.6 %collective-permute-start = (bf16[32,16,128]{2,1,0:T(8,128)(2,1)S(1)}, bf16[32,16,128]{2,1,0:T(8,128)(2,1)S(1)}, u32[]{:S(2)}, u32[]{:S(2)}) collective-permute-start(bf16[32,16,128]{2,1,0:T(8,128)(2,1)S(1)} %copy.38), channel_id=1, source_target_pairs={{0,32},{32,64},{64,96},{96,128},{128,160},{160,192},{192,224},{224... | collective-permute-start | bytes 393224 | tf_op jit(solution)/shard_map/while/body/eval_jaxpr/ppermute | solution.py:43
  513.6 9.8 %collective-permute-start.1 = (f32[32,16,128]{2,1,0:T(8,128)S(1)}, f32[32,16,128]{2,1,0:T(8,128)S(1)}, u32[]{:S(2)}, u32[]{:S(2)}) collective-permute-start(f32[32,16,128]{2,1,0:T(8,128)S(1)} %add.300), channel_id=1, source_target_pairs={{0,32},{32,64},{64,96},{96,128},{128,160},{160,192},{192,224},{224... | collective-permute-start | bytes 786440 | tf_op jit(solution)/shard_map/while/body/eval_jaxpr/ppermute | solution.py:43
  523.4 8.6 %collective-permute-start = (bf16[32,16,128]{2,1,0:T(8,128)(2,1)S(1)}, bf16[32,16,128]{2,1,0:T(8,128)(2,1)S(1)}, u32[]{:S(2)}, u32[]{:S(2)}) collective-permute-start(bf16[32,16,128]{2,1,0:T(8,128)(2,1)S(1)} %copy.38), channel_id=1, source_target_pairs={{0,32},{32,64},{64,96},{96,128},{128,160},{160,192},{192,224},{224... | collective-permute-start | bytes 393224 | tf_op jit(solution)/shard_map/while/body/eval_jaxpr/ppermute | solution.py:43
  529.6 9.8 %collective-permute-start.1 = (f32[32,16,128]{2,1,0:T(8,128)S(1)}, f32[32,16,128]{2,1,0:T(8,128)S(1)}, u32[]{:S(2)}, u32[]{:S(2)}) collective-permute-start(f32[32,16,128]{2,1,0:T(8,128)S(1)} %add.300), channel_id=1, source_target_pairs={{0,32},{32,64},{64,96},{96,128},{128,160},{160,192},{192,224},{224... | collective-permute-start | bytes 786440 | tf_op jit(solution)/shard_map/while/body/eval_jaxpr/ppermute | solution.py:43
  545.6 9.8 %collective-permute-start.1 = (f32[32,16,128]{2,1,0:T(8,128)S(1)}, f32[32,16,128]{2,1,0:T(8,128)S(1)}, u32[]{:S(2)}, u32[]{:S(2)}) collective-permute-start(f32[32,16,128]{2,1,0:T(8,128)S(1)} %add.300), channel_id=1, source_target_pairs={{0,32},{32,64},{64,96},{96,128},{128,160},{160,192},{192,224},{224... | collective-permute-start | bytes 786440 | tf_op jit(solution)/shard_map/while/body/eval_jaxpr/ppermute | solution.py:43
  555.4 8.6 %collective-permute-start = (bf16[32,16,128]{2,1,0:T(8,128)(2,1)S(1)}, bf16[32,16,128]{2,1,0:T(8,128)(2,1)S(1)}, u32[]{:S(2)}, u32[]{:S(2)}) collective-permute-start(bf16[32,16,128]{2,1,0:T(8,128)(2,1)S(1)} %copy.38), channel_id=1, source_target_pairs={{0,32},{32,64},{64,96},{96,128},{128,160},{160,192},{192,224},{224... | collective-permute-start | bytes 393224 | tf_op jit(solution)/shard_map/while/body/eval_jaxpr/ppermute | solution.py:43
  561.7 9.8 %collective-permute-start.1 = (f32[32,16,128]{2,1,0:T(8,128)S(1)}, f32[32,16,128]{2,1,0:T(8,128)S(1)}, u32[]{:S(2)}, u32[]{:S(2)}) collective-permute-start(f32[32,16,128]{2,1,0:T(8,128)S(1)} %add.300), channel_id=1, source_target_pairs={{0,32},{32,64},{64,96},{96,128},{128,160},{160,192},{192,224},{224... | collective-permute-start | bytes 786440 | tf_op jit(solution)/shard_map/while/body/eval_jaxpr/ppermute | solution.py:43
  571.5 8.6 %collective-permute-start = (bf16[32,16,128]{2,1,0:T(8,128)(2,1)S(1)}, bf16[32,16,128]{2,1,0:T(8,128)(2,1)S(1)}, u32[]{:S(2)}, u32[]{:S(2)}) collective-permute-start(bf16[32,16,128]{2,1,0:T(8,128)(2,1)S(1)} %copy.38), channel_id=1, source_target_pairs={{0,32},{32,64},{64,96},{96,128},{128,160},{160,192},{192,224},{224... | collective-permute-start | bytes 393224 | tf_op jit(solution)/shard_map/while/body/eval_jaxpr/ppermute | solution.py:43
  577.7 9.8 %collective-permute-start.1 = (f32[32,16,128]{2,1,0:T(8,128)S(1)}, f32[32,16,128]{2,1,0:T(8,128)S(1)}, u32[]{:S(2)}, u32[]{:S(2)}) collective-permute-start(f32[32,16,128]{2,1,0:T(8,128)S(1)} %add.300), channel_id=1, source_target_pairs={{0,32},{32,64},{64,96},{96,128},{128,160},{160,192},{192,224},{224... | collective-permute-start | bytes 786440 | tf_op jit(solution)/shard_map/while/body/eval_jaxpr/ppermute | solution.py:43
  587.5 8.6 %collective-permute-start = (bf16[32,16,128]{2,1,0:T(8,128)(2,1)S(1)}, bf16[32,16,128]{2,1,0:T(8,128)(2,1)S(1)}, u32[]{:S(2)}, u32[]{:S(2)}) collective-permute-start(bf16[32,16,128]{2,1,0:T(8,128)(2,1)S(1)} %copy.38), channel_id=1, source_target_pairs={{0,32},{32,64},{64,96},{96,128},{128,160},{160,192},{192,224},{224... | collective-permute-start | bytes 393224 | tf_op jit(solution)/shard_map/while/body/eval_jaxpr/ppermute | solution.py:43
  593.7 9.8 %collective-permute-start.1 = (f32[32,16,128]{2,1,0:T(8,128)S(1)}, f32[32,16,128]{2,1,0:T(8,128)S(1)}, u32[]{:S(2)}, u32[]{:S(2)}) collective-permute-start(f32[32,16,128]{2,1,0:T(8,128)S(1)} %add.300), channel_id=1, source_target_pairs={{0,32},{32,64},{64,96},{96,128},{128,160},{160,192},{192,224},{224... | collective-permute-start | bytes 786440 | tf_op jit(solution)/shard_map/while/body/eval_jaxpr/ppermute | solution.py:43
  603.5 8.6 %collective-permute-start = (bf16[32,16,128]{2,1,0:T(8,128)(2,1)S(1)}, bf16[32,16,128]{2,1,0:T(8,128)(2,1)S(1)}, u32[]{:S(2)}, u32[]{:S(2)}) collective-permute-start(bf16[32,16,128]{2,1,0:T(8,128)(2,1)S(1)} %copy.38), channel_id=1, source_target_pairs={{0,32},{32,64},{64,96},{96,128},{128,160},{160,192},{192,224},{224... | collective-permute-start | bytes 393224 | tf_op jit(solution)/shard_map/while/body/eval_jaxpr/ppermute | solution.py:43
  609.7 9.8 %collective-permute-start.1 = (f32[32,16,128]{2,1,0:T(8,128)S(1)}, f32[32,16,128]{2,1,0:T(8,128)S(1)}, u32[]{:S(2)}, u32[]{:S(2)}) collective-permute-start(f32[32,16,128]{2,1,0:T(8,128)S(1)} %add.300), channel_id=1, source_target_pairs={{0,32},{32,64},{64,96},{96,128},{128,160},{160,192},{192,224},{224... | collective-permute-start | bytes 786440 | tf_op jit(solution)/shard_map/while/body/eval_jaxpr/ppermute | solution.py:43
  623.4 9.9 %collective-permute-start.2 = (f32[32,16,128]{2,1,0:T(8,128)S(1)}, f32[32,16,128]{2,1,0:T(8,128)}, u32[]{:S(2)}, u32[]{:S(2)}) collective-permute-start(f32[32,16,128]{2,1,0:T(8,128)S(1)} %add.247), channel_id=1, source_target_pairs={{0,32},{32,64},{64,96},{96,128},{128,160},{160,192},{192,224},{224... | collective-permute-start | bytes 786440 | tf_op jit(solution)/shard_map/ppermute | solution.py:43
  633.3 25.9 %all-to-all-start = ((f32[32,1,16,128]{3,2,1,0:T(8,128)}), f32[32,1,16,128]{3,2,1,0:T(8,128)S(1)}, u32[]{:S(2)}, u32[]{:S(2)}) async-start(f32[32,1,16,128]{3,2,1,0:T(8,128)} %bitcast.32), calls=%async_computation | async-start | bytes 524288 | tf_op jit(solution)/shard_map/all_to_all | solution.py:53
  (18 other events, 297.3 us)
Sparse Core Ops, SparseCore 0:
  94.6 31.2 all-gather.4
where the time goes:
time: 676 us; the launch traced here: 668 us
  blocking collectives  292 us (43%)
  waiting for transfers between devices  135 us (20%)
  matrix products  88 us (13%)
  starting transfers between devices  69.9 us (10%)
  other arithmetic  33.9 us (5%)
  local copies, waits for them, and re-layouts  29.3 us (4%)
  between operations  18 us (3%)
    ppermute x31, waiting for transfers between devices, from_behind(): return lax.ppermute(value, axis, pairs)  117 us
    all_gather x1, blocking collectives, on_device(): lax.all_gather(queries, GROUP, axis=0, tiled=True)  87.3 us
    all_gather x1, blocking collectives, side_by_side(): lax.all_gather(both, axis, axis=dim, tiled=True)  70.5 us
    ppermute x31, starting transfers between devices, from_behind(): return lax.ppermute(value, axis, pairs)  63.5 us
    dot_general x64, matrix products, masked_logits(): lax.dot_general(row_block, lone_document, (((1,), (1,)), ((), ())), prefe...  62.4 us
    pmax x5, blocking collectives, over_axes(): return functools.reduce(lax.pmax, axes, x)  54.4 us
    psum x5, blocking collectives, one_axis_at_a_time(): x = lax.psum(x, axis)  51.7 us
    broadcast_in_dim x32, other arithmetic, masked_logits(): jnp.where(live_image_embeddings[None, :] > 0, similarity_matrix / relaxat...  24.4 us
  transfers between devices with their start and end apart: 33, of which 17 were waited for; matrix products, arithmetic and copies ran while one was open for 11% of the time, Pallas kernels for 0%

commit v1 on v0

v1 whole, which is shorter than its diff:
```python
import jax
import jax.numpy as jnp
from jax import lax
from jax.experimental import pallas as pl
from jax.experimental.pallas import tpu as pltpu
from jax.sharding import Mesh
from jax.sharding import PartitionSpec as P

AXES = ("xl", "y", "c", "xh", "z")
MESH = pl.DeviceIdType.MESH
F32, BF16, I32 = jnp.float32, jnp.bfloat16, jnp.int32
NZ = 16
NS = 16
TOK = 16
D = 128
ROWS = NZ * TOK
STEP = 4
FLOOR = -1e30
MARK = 128.0


def iota(shape, dim):
    return lax.broadcasted_iota(I32, shape, dim)


def exact_dot(a, b):
    return jnp.dot(a, b, preferred_element_type=F32, precision=lax.Precision.HIGHEST)


def kernel(
    q_ref,
    qmask_ref,
    pos_ref,
    pg_ref,
    pmask_ref,
    gq_ref,
    gp_ref,
    loss_ref,
    q_all,
    meta_all,
    pages,
    q_t,
    e_all,
    top,
    tot,
    logn,
    score,
    coef,
    stat,
    gq_t,
    gp_send,
    own_a,
    own_b,
    mid_a,
    mid_b,
    out_a,
    out_b,
    in_a,
    in_b,
    gq_pair,
    gq_in,
    gq_own,
    gq_send,
    gq_recv,
    loss_x,
    loss_y,
    zs_sem,
    q_recv,
    m_recv,
    pair_send,
    pair_recv,
    pg_send,
    pg_recv,
    stat_send,
    stat_recv,
    gp_ssem,
    gp_rsem,
    st2_send,
    st2_recv,
    gq_ssem,
    gq_rsem,
    loss_send,
    loss_recv,
):
    xl, y, c, xh, z = (lax.axis_index(a) for a in AXES)
    x = xh * 2 + xl
    other = 1 - c

    def at_x(d):
        t = lax.rem(x + d, 4)
        return {"xl": lax.rem(t, 2), "xh": lax.div(t, 2)}

    def at_y(d):
        return {"y": lax.rem(y + d, 4)}

    def at_z(d):
        return {"z": lax.rem(z + d, NZ)}

    pair = {"c": other}
    sends = []

    def push(src, dst, ssem, rsem, device):
        copy = pltpu.make_async_remote_copy(
            src_ref=src, dst_ref=dst, send_sem=ssem, recv_sem=rsem, device_id=device, device_id_type=MESH
        )
        copy.start()
        return copy

    def arrived(ref, sem):
        pltpu.make_async_copy(ref, ref, sem).wait()

    barrier = pltpu.get_barrier_semaphore()
    near = [s for d in range(1, STEP + 1) for s in (d, NZ - d)]
    peers = [at_z(d) for d in near] + [pair] + [at_x(d) for d in (1, 2, 3)] + [at_y(d) for d in (1, 2, 3)]
    for device in peers:
        pl.semaphore_signal(barrier, inc=1, device_id=device, device_id_type=MESH)

    prow = iota((128, 128), 0)
    for k in range(2):
        count = jnp.sum(pmask_ref[pl.ds(k, 1), :].astype(F32), axis=1, keepdims=True)
        keep = jnp.logical_or(prow < 127, jnp.broadcast_to(count, (128, 128)) > 127.5)
        pages[0, 0, k] = jnp.where(keep, pg_ref[k].astype(F32), MARK + count).astype(BF16)
    q_all[c, z] = q_ref[0]
    lane = iota((1, 128), 1)
    base = lax.rem(z, 8) * TOK
    meta = jnp.where(lax.shift_right_logical(lane, 4) == lax.rem(z, 8), pos_ref[0] * 2, 0)
    for t in range(TOK):
        meta = meta + jnp.where(lane == base + t, qmask_ref[0, t], 0)
    meta_all[c, z] = meta

    pl.semaphore_wait(barrier, len(peers))

    def send_query(zsrc, d, i):
        sends.append(push(q_all.at[c, zsrc], q_all.at[c, zsrc], zs_sem.at[0, i], q_recv.at[zsrc], at_z(d)))
        sends.append(push(meta_all.at[c, zsrc], meta_all.at[c, zsrc], zs_sem.at[1, i], m_recv.at[zsrc], at_z(d)))

    n = 0
    for d in reversed(near):
        send_query(z, d, n)
        n += 1
    for i, d in enumerate((2, 1, 3)):
        sends.append(push(pages.at[0, 0], pages.at[4 - d, 0], pg_send.at[i], pg_recv.at[0, 4 * (4 - d)], at_x(d)))
        sends.append(push(pages.at[0, 0], pages.at[0, 4 - d], pg_send.at[3 + i], pg_recv.at[0, 4 - d], at_y(d)))
    m = 6
    for d in (1, 3, 2):
        arrived(pages.at[d, 0], pg_recv.at[0, 4 * d])
        for e in (2, 1, 3):
            dst = pages.at[d, 4 - e, 0]
            sends.append(push(pages.at[d, 0, 0], dst, pg_send.at[m], pg_recv.at[0, 4 * d + 4 - e], at_y(e)))
            m += 1
        arrived(pages.at[0, d], pg_recv.at[0, d])
        for e in (2, 1, 3):
            dst = pages.at[4 - e, d, 1]
            sends.append(push(pages.at[0, d, 1], dst, pg_send.at[m], pg_recv.at[1, 4 * (4 - e) + d], at_x(e)))
            m += 1

    def got_query(d):
        zsrc = lax.rem(z + d, NZ)
        arrived(q_all.at[c, zsrc], q_recv.at[zsrc])
        arrived(meta_all.at[c, zsrc], m_recv.at[zsrc])
        return zsrc

    behind = got_query(NZ - STEP)
    for d in range(STEP, 0, -1):
        send_query(behind, d, n)
        n += 1
    ahead = got_query(STEP)
    for d in range(STEP - 1, 0, -1):
        send_query(ahead, NZ - d, n)
        n += 1
    for d in range(1, NZ):
        if d not in (STEP, NZ - STEP):
            got_query(d)
    sends.append(push(q_all.at[c], q_all.at[c], pair_send.at[0], pair_recv.at[0], pair))
    sends.append(push(meta_all.at[c], meta_all.at[c], pair_send.at[1], pair_recv.at[1], pair))
    for dx in range(1, 4):
        for dy in range(1, 4):
            arrived(pages.at[dx, dy, 0], pg_recv.at[0, 4 * dx + dy])
            arrived(pages.at[dx, dy, 1], pg_recv.at[1, 4 * dx + dy])

    def forward(h):
        rows = q_all[h].reshape(ROWS, D)
        q_t[h] = (rows.astype(F32) * 2.0).T.astype(BF16)

        def slot(s, carry):
            rx, ry = lax.div(s, 4), lax.rem(s, 4)
            for k in range(2):
                page = pages[rx, ry, k]
                last = pages[rx, ry, k, pl.ds(112, 16), :].astype(F32)[15:16]
                count = jnp.where(last > 100.0, last - MARK, 128.0)
                count = jnp.concatenate([count, count], axis=1)
                logits = jnp.dot(page, q_t[h], preferred_element_type=F32)
                live = iota((128, ROWS), 0) < count.astype(I32)
                logits = jnp.where(live, logits, FLOOR)
                highest = jnp.max(logits, axis=0, keepdims=True)
                e = jnp.exp(logits - highest)
                e_all[h, s, k] = e
                row = pl.ds(2 * s + k, 1)
                top[h, row, :] = highest
                tot[h, row, :] = jnp.sum(e, axis=0, keepdims=True)
                logn[h, row, :] = count
            return carry

        lax.fori_loop(0, NS, slot, 0)

    forward(c)
    arrived(q_all.at[other], pair_recv.at[0])
    arrived(meta_all.at[other], pair_recv.at[1])
    forward(other)

    same = lax.shift_right_logical(iota((ROWS, ROWS), 0), 4) == lax.shift_right_logical(iota((ROWS, ROWS), 1), 4)
    same = jnp.where(same, 1.0, 0.0).astype(F32)
    i = iota((32, ROWS), 0)
    px = jnp.bitwise_and(x + lax.shift_right_logical(i, 3), 3)
    py = jnp.bitwise_and(y + jnp.bitwise_and(lax.shift_right_logical(i, 1), 3), 3)
    blk = (jnp.bitwise_and(px, 1) * 4 + py) * 2 + c
    page_id = (blk * 32 + lax.shift_right_logical(px, 1) * 16 + z) * 2 + jnp.bitwise_and(i, 1)
    masks, chosen, lse_rows, picked_rows = [], [], [], []
    for h in range(2):
        lo = sum(meta_all[h, t] for t in range(8))
        hi = sum(meta_all[h, t] for t in range(8, 16))
        both = jnp.concatenate([lo, hi], axis=1)
        masks.append(jnp.bitwise_and(both, 1).astype(F32))
        chosen.append(page_id == lax.shift_right_logical(both, 1))
        lse = top[h] + jnp.log(tot[h])
        value = masks[h] * (0.5 * (lse - jnp.log(logn[h])))
        total = exact_dot(value, same)
        score[h] = total
        highest = jnp.max(total, axis=0, keepdims=True)
        lse_rows.append(highest + jnp.log(jnp.sum(jnp.exp(total - highest), axis=0, keepdims=True)))
        picked_rows.append(jnp.sum(jnp.where(chosen[h], total, 0.0), axis=0, keepdims=True))

    tok = jnp.bitwise_and(lane, 15)
    row = jnp.zeros((1, 128), F32)
    for j in range(4):
        part = slice(128 * (j % 2), 128 * (j % 2) + 128)
        piece = jnp.where(tok < 12, lse_rows[j // 2][:, part], picked_rows[j // 2][:, part])
        row = row + jnp.where(jnp.bitwise_and(tok, 3) == j, piece, 0.0)
    mine = c * NZ + z
    stat[mine] = row
    stat_sends = [push(stat.at[mine], stat.at[mine], stat_send.at[0], stat_recv.at[mine], pair)]
    for d in (8, 7, 9, 6, 10, 5, 11, 4, 12, 3, 13, 2, 14, 1, 15):
        for e, cc in ((0, c), (1, other)):
            device = {"c": cc, **at_z(d)}
            stat_sends.append(push(stat.at[mine], stat.at[mine], stat_send.at[2 * d + e], stat_recv.at[mine], device))
    sends += stat_sends
    for d in range(1, NZ):
        for cc in (c, other):
            slot_ = cc * NZ + lax.rem(z + d, NZ)
            arrived(stat.at[slot_], stat_recv.at[slot_])
    slot_ = other * NZ + z
    arrived(stat.at[slot_], stat_recv.at[slot_])
    highest = stat[0]
    for d in range(1, 32):
        highest = jnp.maximum(highest, stat[d])
    total = jnp.zeros((1, 128), F32)
    picked = jnp.zeros((1, 128), F32)
    for d in range(32):
        total = total + jnp.exp(stat[d] - highest)
        picked = picked + stat[d]
    page_lse = highest + jnp.log(total)
    part = jnp.where(tok < 4, page_lse, jnp.where(tok >= 12, -picked, 0.0))
    column_loss = jnp.broadcast_to(jnp.sum(part, axis=1, keepdims=True), (1, 128))
    loss_x[x] = column_loss
    for d in (1, 2, 3):
        sends.append(push(loss_x.at[x], loss_x.at[x], loss_send.at[d], loss_recv.at[x], at_x(d)))
    lane_in, lane_out = iota((128, 512), 0), iota((128, 512), 1)
    source = lax.shift_left(lax.shift_right_logical(jnp.bitwise_and(lane_out, 127), 4), 4) + lax.shift_right_logical(
        lane_out, 7
    )
    spread = jnp.where(lane_in == source, 1.0, 0.0).astype(F32)
    wide = exact_dot(jnp.broadcast_to(page_lse, (8, 128)), spread)[0:1]
    for h in range(2):
        coefficient = jnp.exp(score[h] - wide[:, 256 * h : 256 * h + 256]) - jnp.where(chosen[h], 1.0, 0.0)
        coef[h] = coefficient * masks[h] / tot[h]

    gq_t[...] = jnp.zeros_like(gq_t)

    def gp_copy(s, k, device, dst, rsem):
        return pltpu.make_async_remote_copy(
            src_ref=gp_send.at[s, k],
            dst_ref=dst,
            send_sem=gp_ssem.at[k, s],
            recv_sem=rsem,
            device_id=device,
            device_id_type=MESH,
        )

    def copy_a(s, rx, ry):
        back = lax.rem(4 - ry, 4)
        return gp_copy(s, 0, at_y(ry), mid_a.at[back, rx], gp_rsem.at[0, 4 * back + rx])

    def copy_b(s, rx, ry):
        back = lax.rem(4 - rx, 4)
        return gp_copy(s, 1, at_x(rx), mid_b.at[back, ry], gp_rsem.at[1, 4 * back + ry])

    def backward(t, carry):
        rx = 3 - lax.rem(t, 4)
        ry = 3 - lax.rem(lax.div(t, 4) + lax.rem(t, 4), 4)
        s = 4 * rx + ry
        factors = []
        for h in range(2):
            factors.append(
                [(e_all[h, s, k] * coef[h, pl.ds(2 * s + k, 1), :]).astype(BF16) for k in range(2)]
            )
        grads = []
        for k in range(2):
            g = jnp.dot(factors[0][k], q_all[0].reshape(ROWS, D), preferred_element_type=F32)
            g = g + jnp.dot(factors[1][k], q_all[1].reshape(ROWS, D), preferred_element_type=F32)
            grads.append(g)
            gp_send[s, k] = g.astype(BF16)

        @pl.when(ry != 0)
        def _():
            copy_a(s, rx, ry).start()

        @pl.when(ry == 0)
        def _():
            own_a[rx] = grads[0]

        @pl.when(rx != 0)
        def _():
            copy_b(s, rx, ry).start()

        @pl.when(rx == 0)
        def _():
            own_b[ry] = grads[1]

        page_t = pages[rx, ry].reshape(256, 128).T
        for h in range(2):
            gq_t[h] += jnp.dot(page_t, jnp.concatenate(factors[h], axis=0), preferred_element_type=F32)
        return carry

    lax.fori_loop(0, NS, backward, 0)

    gq_pair[...] = gq_t[other].T
    sends.append(push(gq_pair, gq_in, pair_send.at[2], pair_recv.at[2], pair))
    gq_own[...] = gq_t[c].T

    for d in (1, 2, 3):
        t = lax.rem(x + d, 4)
        arrived(loss_x.at[t], loss_recv.at[t])
    line = loss_x[0] + loss_x[1] + loss_x[2] + loss_x[3]
    loss_y[y] = line
    for d in (1, 2, 3):
        sends.append(push(loss_y.at[y], loss_y.at[y], loss_send.at[4 + d], loss_recv.at[4 + y], at_y(d)))

    arrived(gq_in, pair_recv.at[2])
    gq_own[...] += gq_in[...]
    gq_send[...] = gq_own[...].astype(BF16).reshape(NZ, TOK, D)
    for d in (8, 7, 9, 6, 10, 5, 11, 4, 12, 3, 13, 2, 14, 1, 15):
        zz = lax.rem(z + d, NZ)
        sends.append(push(gq_send.at[zz], gq_recv.at[z], gq_ssem.at[d], gq_rsem.at[z], at_z(d)))

    for r in (2, 1, 3, 0):
        acc_a, acc_b = own_a[r], own_b[r]
        for d in (1, 2, 3):
            arrived(mid_a.at[d, r], gp_rsem.at[0, 4 * d + r])
            acc_a = acc_a + mid_a[d, r].astype(F32)
            arrived(mid_b.at[d, r], gp_rsem.at[1, 4 * d + r])
            acc_b = acc_b + mid_b[d, r].astype(F32)
        if r:
            out_a[r] = acc_a.astype(BF16)
            sends.append(push(out_a.at[r], in_a.at[4 - r], st2_send.at[0, r], st2_recv.at[0, 4 - r], at_x(r)))
            out_b[r] = acc_b.astype(BF16)
            sends.append(push(out_b.at[r], in_b.at[4 - r], st2_send.at[1, r], st2_recv.at[1, 4 - r], at_y(r)))
        else:
            own_a[0] = acc_a
            own_b[0] = acc_b

    for d in (1, 2, 3):
        t = lax.rem(y + d, 4)
        arrived(loss_y.at[t], loss_recv.at[4 + t])
    loss_ref[...] = (loss_y[0] + loss_y[1] + loss_y[2] + loss_y[3]) * (1.0 / 512.0)

    for d in (1, 2, 3):
        arrived(in_a.at[d], st2_recv.at[0, d])
        arrived(in_b.at[d], st2_recv.at[1, d])
    gp_ref[0] = own_a[0] + (in_a[1].astype(F32) + in_a[2].astype(F32) + in_a[3].astype(F32))
    gp_ref[1] = own_b[0] + (in_b[1].astype(F32) + in_b[2].astype(F32) + in_b[3].astype(F32))

    total = gq_own[pl.ds(pl.multiple_of(z * TOK, TOK), TOK), :]
    for d in range(1, NZ):
        zz = lax.rem(z + d, NZ)
        arrived(gq_recv.at[zz], gq_rsem.at[zz])
        total = total + gq_recv[zz].astype(F32)
    gq_ref[0] = total

    for copy in sends:
        copy.wait_send()
    for rx in range(4):
        for ry in range(4):
            s = 4 * rx + ry
            if ry:
                copy_a(s, rx, ry).wait_send()
            if rx:
                copy_b(s, rx, ry).wait_send()


def on_device(queries, query_mask, positive, page_vectors, page_mask):
    vmem = pl.BlockSpec(memory_space=pltpu.VMEM)
    smem = pl.BlockSpec(memory_space=pltpu.SMEM)
    V = pltpu.VMEM
    dma = pltpu.SemaphoreType.DMA
    scratch = [
        V((2, NZ, TOK, D), BF16),
        V((2, NZ, 1, 128), I32),
        V((4, 4, 2, 128, D), BF16),
        V((2, D, ROWS), BF16),
        V((2, NS, 2, 128, ROWS), F32),
        V((2, 32, ROWS), F32),
        V((2, 32, ROWS), F32),
        V((2, 32, ROWS), F32),
        V((2, 32, ROWS), F32),
        V((2, 32, ROWS), F32),
        V((32, 1, 128), F32),
        V((2, D, ROWS), F32),
        V((NS, 2, 128, D), BF16),
        V((4, 128, D), F32),
        V((4, 128, D), F32),
        V((4, 4, 128, D), BF16),
        V((4, 4, 128, D), BF16),
        V((4, 128, D), BF16),
        V((4, 128, D), BF16),
        V((4, 128, D), BF16),
        V((4, 128, D), BF16),
        V((ROWS, D), F32),
        V((ROWS, D), F32),
        V((ROWS, D), F32),
        V((NZ, TOK, D), BF16),
        V((NZ, TOK, D), BF16),
        V((4, 1, 128), F32),
        V((4, 1, 128), F32),
        dma((2, 15)),
        dma((NZ,)),
        dma((NZ,)),
        dma((3,)),
        dma((3,)),
        dma((24,)),
        dma((2, 16)),
        dma((32,)),
        dma((32,)),
        dma((2, 16)),
        dma((2, 16)),
        dma((2, 4)),
        dma((2, 4)),
        dma((NZ,)),
        dma((NZ,)),
        dma((8,)),
        dma((8,)),
    ]
    gq, gp, loss = pl.pallas_call(
        kernel,
        out_shape=(
            jax.ShapeDtypeStruct((1, TOK, D), F32),
            jax.ShapeDtypeStruct((2, 128, D), F32),
            jax.ShapeDtypeStruct((1, 128), F32),
        ),
        in_specs=[vmem, smem, smem, vmem, vmem],
        out_specs=(vmem, vmem, vmem),
        scratch_shapes=scratch,
        compiler_params=pltpu.CompilerParams(collective_id=0, has_side_effects=True),
    )(queries, query_mask, positive, page_vectors, page_mask)
    return gq, gp, loss[0, 0]


def solution(mesh):
    split = Mesh(mesh.devices.reshape(2, 4, 2, 2, 16), AXES)
    return jax.shard_map(
        on_device,
        mesh=split,
        in_specs=(P(AXES, None, None), P(AXES, None), P(AXES), P(AXES, None, None), P(AXES, None)),
        out_specs=(P(AXES, None, None), P(AXES, None, None), P()),
        check_vma=False,
    )
```

time: 676 us -> 66.5 us (0.10)
  the two profiles are of different devices: /device:TPU:2 before, /device:TPU:1 now
where the time goes in v1:
time: 66.5 us; the launch traced here: 66.2 us
  Pallas kernels  60.9 us (92%)
  local copies, waits for them, and re-layouts  2.86 us (4%)
  between operations  2.46 us (4%)
    pallas_call x1, Pallas kernels, on_device(): pl.pallas_call(kernel, out_shape=(jax.ShapeDtypeStruct((1, TOK, D), F32),...  60.9 us
    unnamed x6, local copies, waits for them, and re-layouts  2.86 us

profile of v1, /device:TPU:1, one launch (start us, length us, event | category | flops | bytes accessed | tf_op | source)
XLA Modules:
  0.0 66.2 jit_solution(4130283892358686033)
XLA Ops:
  1.3 60.9 %shard_map.76 = (f32[1,16,128]{2,1,0:T(8,128)}, f32[2,128,128]{2,1,0:T(8,128)}, f32[1,128]{1,0:T(1,128)}) custom-call(bf16[1,16,128]{2,1,0:T(8,128)(2,1)} %q_ref.1, s32[1,16]{1,0:T(1,128)} %qmask_ref.1, s32[1]{0:T(128)S(6)} %copy.11.pos_ref, bf16[2,128,128]{2,1,0:T(8,128)(2,1)} %pg_ref.1, s32[2,128]{1,0:T(2,128)} %pmask_ref.1), custom_call_target="tpu_custom_call" | custom-call | tf_op jit(solution)/shard_map/pallas_call | solution.py:452
  62.2 0.0 copy-start
  62.2 0.7 %copy-done = f32[1,16,128]{2,1,0:T(8,128)S(1)} copy-done((f32[1,16,128]{2,1,0:T(8,128)S(1)}, f32[1,16,128]{2,1,0:T(8,128)}, u32[]{:S(2)}) %copy-start) | copy-done | bytes 8216
  62.9 0.6 copy.12
  63.5 0.0 copy-start.1
  63.5 1.6 %copy.13 = f32[2,128,128]{2,1,0:T(8,128)} copy(f32[2,128,128]{2,1,0:T(8,128)} %get-tuple-element.13) | data formatting | bytes 262144
  65.1 0.0 copy-done.1
Async XLA Ops:
  62.2 0.7 %copy-start = (f32[1,16,128]{2,1,0:T(8,128)S(1)}, f32[1,16,128]{2,1,0:T(8,128)}, u32[]{:S(2)}) copy-start(f32[1,16,128]{2,1,0:T(8,128)} %get-tuple-element.12) | copy-start | bytes 24580
  63.5 1.6 %copy-start.1 = (f32[1,128]{1,0:T(1,128)S(1)}, f32[1,128]{1,0:T(1,128)}, u32[]{:S(2)}) copy-start(f32[1,128]{1,0:T(1,128)} %get-tuple-element.8) | copy-start | bytes 1540

commit v2 on v1

v2 whole, which is shorter than its diff:
```python
import jax
import jax.numpy as jnp
from jax import lax
from jax.experimental import pallas as pl
from jax.experimental.pallas import tpu as pltpu
from jax.sharding import Mesh
from jax.sharding import PartitionSpec as P

AXES = ("xl", "y", "c", "xh", "z")
MESH = pl.DeviceIdType.MESH
F32, BF16, I32 = jnp.float32, jnp.bfloat16, jnp.int32
NZ = 16
NS = 16
TOK = 16
D = 128
ROWS = NZ * TOK
STEP = 4
FLOOR = -1e30
MARK = 128.0


def iota(shape, dim):
    return lax.broadcasted_iota(I32, shape, dim)


def exact_dot(a, b):
    return jnp.dot(a, b, preferred_element_type=F32, precision=lax.Precision.HIGHEST)


def kernel(
    q_hbm,
    qmask_hbm,
    pos_hbm,
    pg_hbm,
    pmask_hbm,
    gq_ref,
    gp_ref,
    loss_ref,
    qmask,
    pos,
    pg_in,
    pmask,
    load_sem,
    q_all,
    meta_all,
    pages,
    pages_t,
    q_t,
    factor,
    e_all,
    top,
    tot,
    logn,
    score,
    coef,
    stat,
    gq_t,
    gp_send,
    own_a,
    own_b,
    mid_a,
    mid_b,
    out_a,
    out_b,
    in_a,
    in_b,
    gq_pair,
    gq_in,
    gq_own,
    gq_send,
    gq_recv,
    loss_x,
    loss_y,
    zs_sem,
    q_recv,
    m_recv,
    pair_send,
    pair_recv,
    pg_send,
    pg_recv,
    stat_send,
    stat_recv,
    gp_ssem,
    gp_rsem,
    st2_send,
    st2_recv,
    gq_ssem,
    gq_rsem,
    loss_send,
    loss_recv,
):
    xl, y, c, xh, z = (lax.axis_index(a) for a in AXES)
    x = xh * 2 + xl
    other = 1 - c

    def at_x(d):
        t = lax.rem(x + d, 4)
        return {"xl": lax.rem(t, 2), "xh": lax.div(t, 2)}

    def at_y(d):
        return {"y": lax.rem(y + d, 4)}

    def at_z(d):
        return {"z": lax.rem(z + d, NZ)}

    pair = {"c": other}
    sends = []

    scopes = []

    def phase(name):
        if scopes:
            scopes.pop().__exit__(None, None, None)
        if name:
            scopes.append(jax.named_scope(name))
            scopes[-1].__enter__()

    def push(src, dst, ssem, rsem, device):
        copy = pltpu.make_async_remote_copy(
            src_ref=src, dst_ref=dst, send_sem=ssem, recv_sem=rsem, device_id=device, device_id_type=MESH
        )
        copy.start()
        return copy

    def arrived(ref, sem):
        pltpu.make_async_copy(ref, ref, sem).wait()

    phase("entry")
    barrier = pltpu.get_barrier_semaphore()
    near = [s for d in range(1, STEP + 1) for s in (d, NZ - d)]
    peers = [at_z(d) for d in near] + [pair] + [at_x(d) for d in (1, 2, 3)] + [at_y(d) for d in (1, 2, 3)]
    for device in peers:
        pl.semaphore_signal(barrier, inc=1, device_id=device, device_id_type=MESH)

    phase("own")
    loads = [
        pltpu.make_async_copy(pg_hbm, pg_in, load_sem.at[0]),
        pltpu.make_async_copy(pmask_hbm, pmask, load_sem.at[1]),
        pltpu.make_async_copy(q_hbm.at[0], q_all.at[c, z], load_sem.at[2]),
        pltpu.make_async_copy(qmask_hbm, qmask, load_sem.at[3]),
        pltpu.make_async_copy(pos_hbm, pos, load_sem.at[4]),
    ]
    for load in loads:
        load.start()
    for load in loads:
        load.wait()
    prow = iota((128, 128), 0)
    for k in range(2):
        count = jnp.sum(pmask[pl.ds(k, 1), :].astype(F32), axis=1, keepdims=True)
        keep = jnp.logical_or(prow < 127, jnp.broadcast_to(count, (128, 128)) > 127.5)
        pages[0, 0, k] = jnp.where(keep, pg_in[k].astype(F32), MARK + count).astype(BF16)
    lane = iota((1, 128), 1)
    base = lax.rem(z, 8) * TOK
    meta = jnp.where(lax.shift_right_logical(lane, 4) == lax.rem(z, 8), pos[0] * 2, 0)
    for t in range(TOK):
        meta = meta + jnp.where(lane == base + t, qmask[0, t], 0)
    meta_all[c, z] = meta

    phase("barrier")
    pl.semaphore_wait(barrier, len(peers))

    phase("issue")

    def send_query(zsrc, d, i):
        sends.append(push(q_all.at[c, zsrc], q_all.at[c, zsrc], zs_sem.at[0, i], q_recv.at[zsrc], at_z(d)))
        sends.append(push(meta_all.at[c, zsrc], meta_all.at[c, zsrc], zs_sem.at[1, i], m_recv.at[zsrc], at_z(d)))

    n = 0
    for i, d in enumerate((2, 1, 3)):
        sends.append(push(pages.at[0, 0], pages.at[4 - d, 0], pg_send.at[i], pg_recv.at[0, 4 * (4 - d)], at_x(d)))
        sends.append(push(pages.at[0, 0], pages.at[0, 4 - d], pg_send.at[3 + i], pg_recv.at[0, 4 - d], at_y(d)))
    for d in reversed(near):
        send_query(z, d, n)
        n += 1

    def got_query(d):
        zsrc = lax.rem(z + d, NZ)
        arrived(q_all.at[c, zsrc], q_recv.at[zsrc])
        arrived(meta_all.at[c, zsrc], m_recv.at[zsrc])
        return zsrc

    phase("query_near")
    behind = got_query(NZ - STEP)
    for d in range(STEP, 0, -1):
        send_query(behind, d, n)
        n += 1
    ahead = got_query(STEP)
    for d in range(STEP - 1, 0, -1):
        send_query(ahead, NZ - d, n)
        n += 1

    phase("relay")
    m = 6
    for d in (1, 3, 2):
        arrived(pages.at[d, 0], pg_recv.at[0, 4 * d])
        for e in (2, 1, 3):
            dst = pages.at[d, 4 - e, 0]
            sends.append(push(pages.at[d, 0, 0], dst, pg_send.at[m], pg_recv.at[0, 4 * d + 4 - e], at_y(e)))
            m += 1
        arrived(pages.at[0, d], pg_recv.at[0, d])
        for e in (2, 1, 3):
            dst = pages.at[4 - e, d, 1]
            sends.append(push(pages.at[0, d, 1], dst, pg_send.at[m], pg_recv.at[1, 4 * (4 - e) + d], at_x(e)))
            m += 1

    phase("query_far")
    for d in range(1, NZ):
        if d not in (STEP, NZ - STEP):
            got_query(d)
    sends.append(push(q_all.at[c], q_all.at[c], pair_send.at[0], pair_recv.at[0], pair))
    sends.append(push(meta_all.at[c], meta_all.at[c], pair_send.at[1], pair_recv.at[1], pair))

    def turn_queries(h):
        q_t[h] = (q_all[h].reshape(ROWS, D).astype(F32) * 2.0).T.astype(BF16)

    def forward(halves, slots):
        for rx, ry in slots:
            s = 4 * rx + ry
            block = pages[rx, ry].reshape(256, D)
            lives = []
            for k in range(2):
                last = pages[rx, ry, k, pl.ds(112, 16), :].astype(F32)[15:16]
                count = jnp.where(last > 100.0, last - MARK, 128.0)
                logn[pl.ds(2 * s + k, 1), :] = count
                lives.append(prow < jnp.broadcast_to(count.astype(I32), (128, 128)))
            for h in halves:
                logits = jnp.dot(block, q_t[h], preferred_element_type=F32)
                for k in range(2):
                    for v in range(2):
                        lanes = pl.ds(128 * v, 128)
                        part = logits[128 * k : 128 * k + 128, 128 * v : 128 * v + 128]
                        part = jnp.where(lives[k], part, FLOOR)
                        highest = jnp.max(part, axis=0, keepdims=True)
                        e = jnp.exp(part - highest)
                        e_all[h, s, k, :, lanes] = e
                        top[h, pl.ds(2 * s + k, 1), lanes] = highest
                        tot[h, pl.ds(2 * s + k, 1), lanes] = jnp.sum(e, axis=0, keepdims=True)

    line_slots = [(0, 0), (1, 0), (0, 1), (3, 0), (0, 3), (2, 0), (0, 2)]
    phase("forward_own")
    turn_queries(c)
    forward([c], line_slots)
    phase("query_pair")
    arrived(q_all.at[other], pair_recv.at[0])
    arrived(meta_all.at[other], pair_recv.at[1])
    phase("forward_other")
    turn_queries(other)
    forward([other], line_slots)
    for dx in (1, 3, 2):
        phase(f"pages_{dx}")
        for dy in range(1, 4):
            arrived(pages.at[dx, dy, 0], pg_recv.at[0, 4 * dx + dy])
            arrived(pages.at[dx, dy, 1], pg_recv.at[1, 4 * dx + dy])
        phase(f"forward_{dx}")
        forward([0, 1], [(dx, dy) for dy in (1, 3, 2)])

    phase("scores")
    same = lax.shift_right_logical(iota((ROWS, ROWS), 0), 4) == lax.shift_right_logical(iota((ROWS, ROWS), 1), 4)
    same = jnp.where(same, 1.0, 0.0).astype(F32)
    i = iota((32, ROWS), 0)
    px = jnp.bitwise_and(x + lax.shift_right_logical(i, 3), 3)
    py = jnp.bitwise_and(y + jnp.bitwise_and(lax.shift_right_logical(i, 1), 3), 3)
    blk = (jnp.bitwise_and(px, 1) * 4 + py) * 2 + c
    page_id = (blk * 32 + lax.shift_right_logical(px, 1) * 16 + z) * 2 + jnp.bitwise_and(i, 1)
    log_count = jnp.log(logn[...])
    log_count = jnp.concatenate([log_count, log_count], axis=1)
    masks, chosen, lse_rows, picked_rows = [], [], [], []
    for h in range(2):
        lo = sum(meta_all[h, t] for t in range(8))
        hi = sum(meta_all[h, t] for t in range(8, 16))
        both = jnp.concatenate([lo, hi], axis=1)
        masks.append(jnp.bitwise_and(both, 1).astype(F32))
        chosen.append(page_id == lax.shift_right_logical(both, 1))
        lse = top[h] + jnp.log(tot[h])
        value = masks[h] * (0.5 * (lse - log_count))
        total = exact_dot(value, same)
        score[h] = total
        highest = jnp.max(total, axis=0, keepdims=True)
        lse_rows.append(highest + jnp.log(jnp.sum(jnp.exp(total - highest), axis=0, keepdims=True)))
        picked_rows.append(jnp.sum(jnp.where(chosen[h], total, 0.0), axis=0, keepdims=True))

    tok = jnp.bitwise_and(lane, 15)
    row = jnp.zeros((1, 128), F32)
    for j in range(4):
        part = slice(128 * (j % 2), 128 * (j % 2) + 128)
        piece = jnp.where(tok < 12, lse_rows[j // 2][:, part], picked_rows[j // 2][:, part])
        row = row + jnp.where(jnp.bitwise_and(tok, 3) == j, piece, 0.0)
    mine = c * NZ + z
    stat[mine] = row
    stat_sends = [push(stat.at[mine], stat.at[mine], stat_send.at[0], stat_recv.at[mine], pair)]
    for d in (8, 7, 9, 6, 10, 5, 11, 4, 12, 3, 13, 2, 14, 1, 15):
        for e, cc in ((0, c), (1, other)):
            device = {"c": cc, **at_z(d)}
            stat_sends.append(push(stat.at[mine], stat.at[mine], stat_send.at[2 * d + e], stat_recv.at[mine], device))
    sends += stat_sends
    phase("turn_pages")
    for s in range(NS):
        pages_t[:, pl.ds(256 * s, 256)] = pages[s // 4, s % 4].reshape(256, D).T
    phase("stat_wait")
    for d in range(1, NZ):
        for cc in (c, other):
            slot_ = cc * NZ + lax.rem(z + d, NZ)
            arrived(stat.at[slot_], stat_recv.at[slot_])
    slot_ = other * NZ + z
    arrived(stat.at[slot_], stat_recv.at[slot_])
    phase("softmax")
    highest = stat[0]
    for d in range(1, 32):
        highest = jnp.maximum(highest, stat[d])
    total = jnp.zeros((1, 128), F32)
    picked = jnp.zeros((1, 128), F32)
    for d in range(32):
        total = total + jnp.exp(stat[d] - highest)
        picked = picked + stat[d]
    page_lse = highest + jnp.log(total)
    part = jnp.where(tok < 4, page_lse, jnp.where(tok >= 12, -picked, 0.0))
    column_loss = jnp.broadcast_to(jnp.sum(part, axis=1, keepdims=True), (1, 128))
    loss_x[x] = column_loss
    for d in (1, 2, 3):
        sends.append(push(loss_x.at[x], loss_x.at[x], loss_send.at[d], loss_recv.at[x], at_x(d)))
    lane_in, lane_out = iota((128, 512), 0), iota((128, 512), 1)
    source = lax.shift_left(lax.shift_right_logical(jnp.bitwise_and(lane_out, 127), 4), 4) + lax.shift_right_logical(
        lane_out, 7
    )
    spread = jnp.where(lane_in == source, 1.0, 0.0).astype(F32)
    wide = exact_dot(jnp.broadcast_to(page_lse, (8, 128)), spread)[0:1]
    for h in range(2):
        coefficient = jnp.exp(score[h] - wide[:, 256 * h : 256 * h + 256]) - jnp.where(chosen[h], 1.0, 0.0)
        coef[h] = coefficient * masks[h] / tot[h]

    phase("backward")
    queries = q_all[...].reshape(2 * ROWS, D)
    for rx in (2, 1, 3, 0):
        for ry in (2, 1, 3, 0):
            s = 4 * rx + ry
            rows = pl.ds(256 * s, 256)
            for h in range(2):
                for k in range(2):
                    value = e_all[h, s, k] * coef[h, pl.ds(2 * s + k, 1), :]
                    factor[pl.ds(256 * s + 128 * k, 128), pl.ds(ROWS * h, ROWS)] = value.astype(BF16)
            grads = jnp.dot(factor[rows, :], queries, preferred_element_type=F32)
            grads_a, grads_b = grads[:128], grads[128:]
            if ry:
                gp_send[s, 0] = grads_a.astype(BF16)
                rsem = gp_rsem.at[0, 4 * (4 - ry) + rx]
                sends.append(push(gp_send.at[s, 0], mid_a.at[4 - ry, rx], gp_ssem.at[0, s], rsem, at_y(ry)))
            else:
                own_a[rx] = grads_a
            if rx:
                gp_send[s, 1] = grads_b.astype(BF16)
                rsem = gp_rsem.at[1, 4 * (4 - rx) + ry]
                sends.append(push(gp_send.at[s, 1], mid_b.at[4 - rx, ry], gp_ssem.at[1, s], rsem, at_x(rx)))
            else:
                own_b[ry] = grads_b
    phase("grad_queries")
    for h in range(2):
        gq_t[h] = jnp.dot(pages_t[...], factor[:, pl.ds(ROWS * h, ROWS)], preferred_element_type=F32)

    phase("turn")
    gq_pair[...] = gq_t[other].T
    sends.append(push(gq_pair, gq_in, pair_send.at[2], pair_recv.at[2], pair))
    gq_own[...] = gq_t[c].T

    phase("loss_line")
    for d in (1, 2, 3):
        t = lax.rem(x + d, 4)
        arrived(loss_x.at[t], loss_recv.at[t])
    line = loss_x[0] + loss_x[1] + loss_x[2] + loss_x[3]
    loss_y[y] = line
    for d in (1, 2, 3):
        sends.append(push(loss_y.at[y], loss_y.at[y], loss_send.at[4 + d], loss_recv.at[4 + y], at_y(d)))

    phase("gq_pair")
    arrived(gq_in, pair_recv.at[2])
    gq_own[...] += gq_in[...]
    gq_send[...] = gq_own[...].astype(BF16).reshape(NZ, TOK, D)
    for d in (8, 7, 9, 6, 10, 5, 11, 4, 12, 3, 13, 2, 14, 1, 15):
        zz = lax.rem(z + d, NZ)
        sends.append(push(gq_send.at[zz], gq_recv.at[z], gq_ssem.at[d], gq_rsem.at[z], at_z(d)))

    phase("lines")
    for r in (2, 1, 3, 0):
        acc_a, acc_b = own_a[r], own_b[r]
        for d in (1, 2, 3):
            arrived(mid_a.at[d, r], gp_rsem.at[0, 4 * d + r])
            acc_a = acc_a + mid_a[d, r].astype(F32)
            arrived(mid_b.at[d, r], gp_rsem.at[1, 4 * d + r])
            acc_b = acc_b + mid_b[d, r].astype(F32)
        if r:
            out_a[r] = acc_a.astype(BF16)
            sends.append(push(out_a.at[r], in_a.at[4 - r], st2_send.at[0, r], st2_recv.at[0, 4 - r], at_x(r)))
            out_b[r] = acc_b.astype(BF16)
            sends.append(push(out_b.at[r], in_b.at[4 - r], st2_send.at[1, r], st2_recv.at[1, 4 - r], at_y(r)))
        else:
            own_a[0] = acc_a
            own_b[0] = acc_b

    phase("loss")
    for d in (1, 2, 3):
        t = lax.rem(y + d, 4)
        arrived(loss_y.at[t], loss_recv.at[4 + t])
    loss_ref[...] = (loss_y[0] + loss_y[1] + loss_y[2] + loss_y[3]) * (1.0 / 512.0)

    phase("gp_last")
    for d in (1, 2, 3):
        arrived(in_a.at[d], st2_recv.at[0, d])
        arrived(in_b.at[d], st2_recv.at[1, d])
    gp_ref[0] = own_a[0] + (in_a[1].astype(F32) + in_a[2].astype(F32) + in_a[3].astype(F32))
    gp_ref[1] = own_b[0] + (in_b[1].astype(F32) + in_b[2].astype(F32) + in_b[3].astype(F32))

    phase("gq_last")
    total = gq_own[pl.ds(pl.multiple_of(z * TOK, TOK), TOK), :]
    for d in range(1, NZ):
        zz = lax.rem(z + d, NZ)
        arrived(gq_recv.at[zz], gq_rsem.at[zz])
        total = total + gq_recv[zz].astype(F32)
    gq_ref[0] = total

    phase("drain")
    for copy in sends:
        copy.wait_send()
    phase(None)


def write_out(gq_in, gp_in, loss_in, gq_hbm, gp_hbm, loss_out, sem):
    copies = [
        pltpu.make_async_copy(gp_in, gp_hbm, sem.at[0]),
        pltpu.make_async_copy(gq_in, gq_hbm, sem.at[1]),
    ]
    for copy in copies:
        copy.start()
    loss_out[0] = loss_in[0, 0]
    for copy in copies:
        copy.wait()


def on_device(queries, query_mask, positive, page_vectors, page_mask):
    hbm = pl.BlockSpec(memory_space=pl.ANY)
    vmem = pl.BlockSpec(memory_space=pltpu.VMEM)
    smem = pl.BlockSpec(memory_space=pltpu.SMEM)
    V = pltpu.VMEM
    dma = pltpu.SemaphoreType.DMA
    scratch = [
        pltpu.SMEM((1, TOK), I32),
        pltpu.SMEM((1,), I32),
        V((2, 128, D), BF16),
        V((2, 128), I32),
        dma((5,)),
        V((2, NZ, TOK, D), BF16),
        V((2, NZ, 1, 128), I32),
        V((4, 4, 2, 128, D), BF16),
        V((D, NS * 256), BF16),
        V((2, D, ROWS), BF16),
        V((NS * 256, 2 * ROWS), BF16),
        V((2, NS, 2, 128, ROWS), F32),
        V((2, 32, ROWS), F32),
        V((2, 32, ROWS), F32),
        V((32, 128), F32),
        V((2, 32, ROWS), F32),
        V((2, 32, ROWS), F32),
        V((32, 1, 128), F32),
        V((2, D, ROWS), F32),
        V((NS, 2, 128, D), BF16),
        V((4, 128, D), F32),
        V((4, 128, D), F32),
        V((4, 4, 128, D), BF16),
        V((4, 4, 128, D), BF16),
        V((4, 128, D), BF16),
        V((4, 128, D), BF16),
        V((4, 128, D), BF16),
        V((4, 128, D), BF16),
        V((ROWS, D), F32),
        V((ROWS, D), F32),
        V((ROWS, D), F32),
        V((NZ, TOK, D), BF16),
        V((NZ, TOK, D), BF16),
        V((4, 1, 128), F32),
        V((4, 1, 128), F32),
        dma((2, 15)),
        dma((NZ,)),
        dma((NZ,)),
        dma((3,)),
        dma((3,)),
        dma((24,)),
        dma((2, 16)),
        dma((32,)),
        dma((32,)),
        dma((2, 16)),
        dma((2, 16)),
        dma((2, 4)),
        dma((2, 4)),
        dma((NZ,)),
        dma((NZ,)),
        dma((8,)),
        dma((8,)),
    ]
    partial = pl.pallas_call(
        kernel,
        out_shape=(V((1, TOK, D), F32), V((2, 128, D), F32), V((1, 128), F32)),
        in_specs=[hbm] * 5,
        out_specs=(vmem, vmem, vmem),
        scratch_shapes=scratch,
        compiler_params=pltpu.CompilerParams(collective_id=0, has_side_effects=True),
    )(queries, query_mask, positive, page_vectors, page_mask)
    gq, gp, loss = pl.pallas_call(
        write_out,
        out_shape=(
            jax.ShapeDtypeStruct((1, TOK, D), F32),
            jax.ShapeDtypeStruct((2, 128, D), F32),
            jax.ShapeDtypeStruct((1,), F32),
        ),
        in_specs=[vmem] * 3,
        out_specs=(hbm, hbm, smem),
        scratch_shapes=[dma((2,))],
        compiler_params=pltpu.CompilerParams(vmem_limit_bytes=1 << 20),
    )(*[pltpu.with_memory_space_constraint(p, pltpu.VMEM) for p in partial])
    return gq, gp, loss.reshape(())


def solution(mesh):
    split = Mesh(mesh.devices.reshape(2, 4, 2, 2, 16), AXES)
    return jax.shard_map(
        on_device,
        mesh=split,
        in_specs=(P(AXES, None, None), P(AXES, None), P(AXES), P(AXES, None, None), P(AXES, None)),
        out_specs=(P(AXES, None, None), P(AXES, None, None), P()),
        check_vma=False,
    )
```

time: 66.5 us -> 51.9 us (0.78)
  Pallas kernels: 60.9 us -> 50.5 us
  local copies, waits for them, and re-layouts: 2.86 us -> 0 us
  between operations: 2.46 us -> 1.28 us
    pallas_call x1 -> x2, Pallas kernels: 60.9 us -> 50.5 us  [the longest x1 49.3 us: on_device(): pl.pallas_call(kernel, out_shape=(V((1, TOK, D), F32), V((2, 128, D), F32...]
    unnamed x6 -> x0, local copies, waits for them, and re-layouts: 2.86 us -> none
where the time goes in v2:
time: 51.9 us; the launch traced here: 51.7 us
  Pallas kernels  50.5 us (97%)
  between operations  1.28 us (2%)
    pallas_call x1, Pallas kernels, on_device(): pl.pallas_call(kernel, out_shape=(V((1, TOK, D), F32), V((2, 128, D), F32...  49.3 us
    pallas_call x1, Pallas kernels, on_device(): pl.pallas_call(write_out, out_shape=(jax.ShapeDtypeStruct((1, TOK, D), F3...  1.19 us

profile of v2, /device:TPU:1, one launch (start us, length us, event | category | flops | bytes accessed | tf_op | source)
XLA Modules:
  0.0 51.7 jit_solution(215204326370802260)
XLA Ops:
  1.3 49.3 %shard_map.76 = (f32[1,16,128]{2,1,0:T(8,128)S(1)}, f32[2,128,128]{2,1,0:T(8,128)S(1)}, f32[1,128]{1,0:T(1,128)S(1)}) custom-call(bf16[1,16,128]{2,1,0:T(8,128)(2,1)} %q_hbm.1, s32[1,16]{1,0:T(1,128)} %qmask_hbm.1, s32[1]{0:T(128)S(6)} %copy.8.pos_hbm, bf16[2,128,128]{2,1,0:T(8,128)(2,1)} %pg_hbm.1, s32[2,128]{1,0:T(2,128)} %pmask_hbm.1), custom_call_target="tpu_custom_call" | custom-call | tf_op jit(solution)/shard_map/pallas_call | solution.py:497
  50.6 1.2 %shard_map.77 = (f32[1,16,128]{2,1,0:T(8,128)}, f32[2,128,128]{2,1,0:T(8,128)}, f32[1]{0:T(128)}) custom-call(f32[1,16,128]{2,1,0:T(8,128)S(1)} %get-tuple-element.9.gq_in, f32[2,128,128]{2,1,0:T(8,128)S(1)} %get-tuple-element.10.gp_in, f32[1,128]{1,0:T(1,128)S(1)} %get-tuple-element.11.loss_in), custom_call_target="tpu_custom_call" | custom-call | tf_op jit(solution)/shard_map/pallas_call | solution.py:505

commit v3 on v2

v3 whole, which is shorter than its diff:
```python
import jax
import jax.numpy as jnp
from jax import lax
from jax.experimental import pallas as pl
from jax.experimental.pallas import tpu as pltpu
from jax.sharding import Mesh
from jax.sharding import PartitionSpec as P

AXES = ("xl", "y", "c", "xh", "z")
MESH = pl.DeviceIdType.MESH
F32, BF16, I32 = jnp.float32, jnp.bfloat16, jnp.int32
NZ = 16
NS = 16
TOK = 16
D = 128
ROWS = NZ * TOK
STEP = 4
FLOOR = -1e30
MARK = 128.0


def iota(shape, dim):
    return lax.broadcasted_iota(I32, shape, dim)


def exact_dot(a, b):
    return jnp.dot(a, b, preferred_element_type=F32, precision=lax.Precision.HIGHEST)


def kernel(
    q_hbm,
    qmask_hbm,
    pos_hbm,
    pg_hbm,
    pmask_hbm,
    gq_ref,
    gp_ref,
    loss_ref,
    qmask,
    pos,
    pg_in,
    pmask,
    load_sem,
    q_all,
    pages,
    pages_t,
    q_t,
    factor,
    e_all,
    top,
    tot,
    logn,
    score,
    coef,
    stat,
    gq_t,
    gp_send,
    own_a,
    own_b,
    mid_a,
    mid_b,
    out_a,
    out_b,
    in_a,
    in_b,
    gq_pair,
    gq_in,
    gq_own,
    gq_send,
    gq_recv,
    loss_x,
    loss_y,
    q_send,
    q_recv,
    pair_send,
    pair_recv,
    pg_send,
    line_recv,
    far_recv,
    stat_sem,
    gp_send_sem,
    gp_recv,
    st2_send,
    st2_recv,
    gq_sem,
    loss_sem,
):
    xl, y, c, xh, z = (lax.axis_index(a) for a in AXES)
    x = xh * 2 + xl
    other = 1 - c

    def at_x(d):
        t = lax.rem(x + d, 4)
        return {"xl": lax.rem(t, 2), "xh": lax.div(t, 2)}

    def at_y(d):
        return {"y": lax.rem(y + d, 4)}

    def at_z(d):
        return {"z": lax.rem(z + d, NZ)}

    pair = {"c": other}

    scopes = []

    def phase(name):
        if scopes:
            scopes.pop().__exit__(None, None, None)
        if name:
            scopes.append(jax.named_scope(name))
            scopes[-1].__enter__()

    def push(src, dst, ssem, rsem, device):
        copy = pltpu.make_async_remote_copy(
            src_ref=src, dst_ref=dst, send_sem=ssem, recv_sem=rsem, device_id=device, device_id_type=MESH
        )
        copy.start()

    def arrived(ref, sem):
        pltpu.make_async_copy(ref, ref, sem).wait()

    phase("entry")
    barrier = pltpu.get_barrier_semaphore()
    near = [s for d in range(1, STEP + 1) for s in (d, NZ - d)]
    peers = [at_z(d) for d in near] + [pair] + [at_x(d) for d in (1, 2, 3)] + [at_y(d) for d in (1, 2, 3)]
    for device in peers:
        pl.semaphore_signal(barrier, inc=1, device_id=device, device_id_type=MESH)

    phase("own")
    loads = [
        pltpu.make_async_copy(pg_hbm, pg_in, load_sem.at[0]),
        pltpu.make_async_copy(pmask_hbm, pmask, load_sem.at[1]),
        pltpu.make_async_copy(q_hbm.at[0], q_all.at[c, z, pl.ds(0, TOK)], load_sem.at[2]),
        pltpu.make_async_copy(qmask_hbm, qmask, load_sem.at[3]),
        pltpu.make_async_copy(pos_hbm, pos, load_sem.at[4]),
    ]
    for load in loads:
        load.start()
    for load in loads:
        load.wait()
    prow = iota((128, 128), 0)
    for k in range(2):
        count = jnp.sum(pmask[pl.ds(k, 1), :].astype(F32), axis=1, keepdims=True)
        keep = jnp.logical_or(prow < 127, jnp.broadcast_to(count, (128, 128)) > 127.5)
        pages[0, k] = jnp.where(keep, pg_in[k].astype(F32), MARK + count).astype(BF16)
    lane = iota((1, 128), 1)
    base = lax.rem(z, 8) * TOK
    mask = jnp.zeros((1, 128), I32)
    for t in range(TOK):
        mask = mask + jnp.where(lane == base + t, qmask[0, t], 0)
    group = lax.shift_right_logical(lane, 4) == lax.rem(z, 8)
    page_hi = jnp.where(group, lax.shift_right_logical(pos[0, 0], 5), 0)
    page_lo = jnp.where(group, jnp.bitwise_and(pos[0, 0], 31), 0)
    mrow = iota((8, 128), 0)
    meta = jnp.where(mrow == 0, mask, jnp.where(mrow == 1, page_hi, jnp.where(mrow == 2, page_lo, 0)))
    q_all[c, z, pl.ds(TOK, 8), :] = meta.astype(F32).astype(BF16)

    phase("barrier")
    pl.semaphore_wait(barrier, len(peers))

    phase("issue")

    def send_query(zsrc, d, i):
        push(q_all.at[c, zsrc], q_all.at[c, zsrc], q_send, q_recv.at[i], at_z(d))

    for d in (2, 1, 3):
        push(pages.at[0, 0], pages.at[4 * (4 - d), 0], pg_send, line_recv.at[0, d - 1], at_x(d))
        push(pages.at[0, 1], pages.at[4 - d, 1], pg_send, line_recv.at[1, d - 1], at_y(d))
    for d in (2, 1, 3):
        push(pages.at[0, 1], pages.at[4 * (4 - d), 1], pg_send, far_recv.at[0], at_x(d))
        push(pages.at[0, 0], pages.at[4 - d, 0], pg_send, far_recv.at[0], at_y(d))

    for d in reversed(near):
        send_query(z, d, 0 if d == STEP else 1 if d == NZ - STEP else 2)

    def got_query(d, i):
        zsrc = lax.rem(z + d, NZ)
        arrived(q_all.at[c, zsrc], q_recv.at[i])
        return zsrc

    phase("relay")
    for d in (1, 3, 2):
        arrived(pages.at[4 * d, 0], line_recv.at[0, 3 - d])
        for e in (2, 1, 3):
            push(pages.at[4 * d, 0], pages.at[4 * d + 4 - e, 0], pg_send, far_recv.at[d], at_y(e))
        arrived(pages.at[d, 1], line_recv.at[1, 3 - d])
        for e in (2, 1, 3):
            push(pages.at[d, 1], pages.at[4 * (4 - e) + d, 1], pg_send, far_recv.at[4 - e], at_x(e))

    phase("query_near")
    behind = got_query(NZ - STEP, 0)
    for d in range(STEP, 0, -1):
        send_query(behind, d, 2)
    ahead = got_query(STEP, 1)
    for d in range(STEP - 1, 0, -1):
        send_query(ahead, NZ - d, 2)

    phase("query_far")
    arrived(q_all.at[c, pl.ds(0, 13)], q_recv.at[2])
    push(q_all.at[c], q_all.at[c], pair_send.at[0], pair_recv.at[0], pair)

    def turn_queries(h):
        q_t[h] = (q_all[h, :, pl.ds(0, TOK), :].reshape(ROWS, D).astype(F32) * 2.0).T.astype(BF16)

    def forward(h, slots):
        for rx, ry in slots:
            s = 4 * rx + ry
            for k in range(2):
                last = pages[s, k, pl.ds(112, 16), :].astype(F32)[15:16]
                count = jnp.where(last > 100.0, last - MARK, 128.0)
                live = prow < jnp.broadcast_to(count.astype(I32), (128, 128))
                row = pl.ds(2 * s + k, 1)
                logn[row, :] = count
                logits = jnp.dot(pages[s, k], q_t[h], preferred_element_type=F32)
                for v in range(2):
                    lanes = pl.ds(128 * v, 128)
                    part = jnp.where(live, logits[:, 128 * v : 128 * v + 128], FLOOR)
                    highest = jnp.max(part, axis=0, keepdims=True)
                    e = jnp.exp(part - highest)
                    e_all[h, s, k, :, lanes] = e
                    top[h, row, lanes] = highest
                    tot[h, row, lanes] = jnp.sum(e, axis=0, keepdims=True)

    line_slots = [(0, 0), (1, 0), (0, 1), (3, 0), (0, 3), (2, 0), (0, 2)]
    far_slots = [(dx, dy) for dx in (1, 3, 2) for dy in (1, 3, 2)]
    phase("forward_own")
    turn_queries(c)
    arrived(pages.at[pl.ds(0, 3)], far_recv.at[0])
    forward(c, line_slots)
    phase("pages_far")
    for dx in (1, 2, 3):
        arrived(pages.at[pl.ds(4 * dx + 1, 3)], far_recv.at[dx])
    phase("forward_far")
    forward(c, far_slots)
    phase("query_pair")
    arrived(q_all.at[other], pair_recv.at[0])
    phase("forward_other")
    turn_queries(other)
    forward(other, line_slots + far_slots)

    phase("scores")
    same = lax.shift_right_logical(iota((ROWS, ROWS), 0), 4) == lax.shift_right_logical(iota((ROWS, ROWS), 1), 4)
    same = jnp.where(same, 1.0, 0.0).astype(F32)
    i = iota((32, ROWS), 0)
    px = jnp.bitwise_and(x + lax.shift_right_logical(i, 3), 3)
    py = jnp.bitwise_and(y + jnp.bitwise_and(lax.shift_right_logical(i, 1), 3), 3)
    blk = (jnp.bitwise_and(px, 1) * 4 + py) * 2 + c
    page_id = (blk * 32 + lax.shift_right_logical(px, 1) * 16 + z) * 2 + jnp.bitwise_and(i, 1)
    log_count = jnp.log(logn[...])
    log_count = jnp.concatenate([log_count, log_count], axis=1)
    masks, chosen, lse_rows, picked_rows = [], [], [], []
    for h in range(2):
        lo = sum(q_all[h, t, pl.ds(TOK, 8), :].astype(F32) for t in range(8))
        hi = sum(q_all[h, t, pl.ds(TOK, 8), :].astype(F32) for t in range(8, 16))
        both = jnp.concatenate([lo, hi], axis=1)
        masks.append(both[0:1])
        chosen.append(page_id.astype(F32) == both[1:2] * 32.0 + both[2:3])
        lse = top[h] + jnp.log(tot[h])
        value = masks[h] * (0.5 * (lse - log_count))
        total = exact_dot(value, same)
        score[h] = total
        highest = jnp.max(total, axis=0, keepdims=True)
        lse_rows.append(highest + jnp.log(jnp.sum(jnp.exp(total - highest), axis=0, keepdims=True)))
        picked_rows.append(jnp.sum(jnp.where(chosen[h], total, 0.0), axis=0, keepdims=True))

    tok = jnp.bitwise_and(lane, 15)
    row = jnp.zeros((1, 128), F32)
    for j in range(4):
        part = slice(128 * (j % 2), 128 * (j % 2) + 128)
        piece = jnp.where(tok < 12, lse_rows[j // 2][:, part], picked_rows[j // 2][:, part])
        row = row + jnp.where(jnp.bitwise_and(tok, 3) == j, piece, 0.0)
    mine = c * NZ + z
    stat[mine] = row
    push(stat.at[mine], stat.at[mine], stat_sem.at[0], stat_sem.at[1], pair)
    for d in (8, 7, 9, 6, 10, 5, 11, 4, 12, 3, 13, 2, 14, 1, 15):
        for cc in (c, other):
            push(stat.at[mine], stat.at[mine], stat_sem.at[0], stat_sem.at[1], {"c": cc, **at_z(d)})
    order = []
    for r in (2, 1, 3, 0):
        for d in (2, 1, 3):
            order += [(4 * r + d, 0), (4 * d + r, 1)]
    order += [(4 * r, 0) for r in range(4)] + [(r, 1) for r in range(4)]
    phase("turn_pages")
    for i, (s, k) in enumerate(order):
        pages_t[:, pl.ds(128 * i, 128)] = pages[s, k].T
    phase("stat_wait")
    arrived(stat.at[pl.ds(0, 31)], stat_sem.at[1])
    phase("softmax")
    highest = stat[0]
    for d in range(1, 32):
        highest = jnp.maximum(highest, stat[d])
    total = jnp.zeros((1, 128), F32)
    picked = jnp.zeros((1, 128), F32)
    for d in range(32):
        total = total + jnp.exp(stat[d] - highest)
        picked = picked + stat[d]
    page_lse = highest + jnp.log(total)
    part = jnp.where(tok < 4, page_lse, jnp.where(tok >= 12, -picked, 0.0))
    column_loss = jnp.broadcast_to(jnp.sum(part, axis=1, keepdims=True), (1, 128))
    loss_x[x] = column_loss
    for d in (1, 2, 3):
        push(loss_x.at[x], loss_x.at[x], loss_sem.at[0], loss_sem.at[1], at_x(d))
    lane_in, lane_out = iota((128, 512), 0), iota((128, 512), 1)
    source = lax.shift_left(lax.shift_right_logical(jnp.bitwise_and(lane_out, 127), 4), 4) + lax.shift_right_logical(
        lane_out, 7
    )
    spread = jnp.where(lane_in == source, 1.0, 0.0).astype(F32)
    wide = exact_dot(jnp.broadcast_to(page_lse, (8, 128)), spread)[0:1]
    for h in range(2):
        coefficient = jnp.exp(score[h] - wide[:, 256 * h : 256 * h + 256]) - jnp.where(chosen[h], 1.0, 0.0)
        coef[h] = coefficient * masks[h] / tot[h]

    phase("backward")
    queries = q_all[:, :, pl.ds(0, TOK), :].reshape(2 * ROWS, D)

    def form_factor(i):
        s, k = order[i]
        for h in range(2):
            value = e_all[h, s, k] * coef[h, pl.ds(2 * s + k, 1), :]
            factor[pl.ds(128 * i, 128), pl.ds(ROWS * h, ROWS)] = value.astype(BF16)

    def page_grads(start, size):
        grads = jnp.dot(factor[pl.ds(128 * start, 128 * size), :], queries, preferred_element_type=F32)
        for i in range(size):
            s, k = order[start + i]
            rx, ry = s // 4, s % 4
            g = grads[128 * i : 128 * i + 128]
            if k == 0 and ry:
                gp_send[s, 0] = g.astype(BF16)
                push(gp_send.at[s, 0], mid_a.at[rx, 3 - ry], gp_send_sem, gp_recv.at[0, rx], at_y(ry))
            elif k == 0:
                own_a[rx] = g
            elif rx:
                gp_send[s, 1] = g.astype(BF16)
                push(gp_send.at[s, 1], mid_b.at[ry, 3 - rx], gp_send_sem, gp_recv.at[1, ry], at_x(rx))
            else:
                own_b[ry] = g

    def query_grads():
        for h in range(2):
            gq_t[h] = jnp.dot(pages_t[...], factor[:, pl.ds(ROWS * h, ROWS)], preferred_element_type=F32)
        gq_pair[...] = gq_t[other].T
        push(gq_pair, gq_in, pair_send.at[1], pair_recv.at[1], pair)
        gq_own[...] = gq_t[c].T

    def query_grads_away():
        arrived(gq_in, pair_recv.at[1])
        gq_own[...] += gq_in[...]
        gq_send[...] = gq_own[...].astype(BF16).reshape(NZ, TOK, D)
        for d in (8, 7, 9, 6, 10, 5, 11, 4, 12, 3, 13, 2, 14, 1, 15):
            zz = lax.rem(z + d, NZ)
            push(gq_send.at[zz], gq_recv.at[z], gq_sem.at[0], gq_sem.at[1], at_z(d))

    @pl.when(z < 4)
    def _():
        for start in range(0, 32, 4):
            for i in range(4):
                form_factor(start + i)
            page_grads(start, 4)
        query_grads()
        query_grads_away()

    @pl.when(z >= 4)
    def _():
        for i in range(32):
            form_factor(i)
        query_grads()
        for start in range(0, 16, 4):
            page_grads(start, 4)
        query_grads_away()
        for start in range(16, 32, 4):
            page_grads(start, 4)

    phase("loss_line")
    arrived(loss_x.at[pl.ds(0, 3)], loss_sem.at[1])
    line = loss_x[0] + loss_x[1] + loss_x[2] + loss_x[3]
    loss_y[y] = line
    for d in (1, 2, 3):
        push(loss_y.at[y], loss_y.at[y], loss_sem.at[2], loss_sem.at[3], at_y(d))

    phase("lines")
    for r in (2, 1, 3, 0):
        arrived(mid_a.at[r], gp_recv.at[0, r])
        acc_a = own_a[r] + (mid_a[r, 0].astype(F32) + mid_a[r, 1].astype(F32) + mid_a[r, 2].astype(F32))
        arrived(mid_b.at[r], gp_recv.at[1, r])
        acc_b = own_b[r] + (mid_b[r, 0].astype(F32) + mid_b[r, 1].astype(F32) + mid_b[r, 2].astype(F32))
        if r:
            out_a[r - 1] = acc_a.astype(BF16)
            push(out_a.at[r - 1], in_a.at[3 - r], st2_send.at[0], st2_recv.at[0], at_x(r))
            out_b[r - 1] = acc_b.astype(BF16)
            push(out_b.at[r - 1], in_b.at[3 - r], st2_send.at[1], st2_recv.at[1], at_y(r))
        else:
            own_a[0] = acc_a
            own_b[0] = acc_b

    phase("loss")
    arrived(loss_y.at[pl.ds(0, 3)], loss_sem.at[3])
    loss_ref[...] = (loss_y[0] + loss_y[1] + loss_y[2] + loss_y[3]) * (1.0 / 512.0)

    phase("gp_last")
    arrived(in_a, st2_recv.at[0])
    gp_ref[0] = own_a[0] + (in_a[0].astype(F32) + in_a[1].astype(F32) + in_a[2].astype(F32))
    arrived(in_b, st2_recv.at[1])
    gp_ref[1] = own_b[0] + (in_b[0].astype(F32) + in_b[1].astype(F32) + in_b[2].astype(F32))

    phase("gq_last")
    total = gq_own[pl.ds(pl.multiple_of(z * TOK, TOK), TOK), :]
    arrived(gq_recv.at[pl.ds(0, NZ - 1)], gq_sem.at[1])
    for d in range(1, NZ):
        zz = lax.rem(z + d, NZ)
        total = total + gq_recv[zz].astype(F32)
    gq_ref[0] = total

    phase("drain")
    arrived(q_all.at[c, pl.ds(0, NZ - 1)], q_send)
    arrived(pages.at[pl.ds(0, NS - 1)], pg_send)
    arrived(q_all.at[c], pair_send.at[0])
    arrived(gq_pair, pair_send.at[1])
    arrived(stat.at[pl.ds(0, 31)], stat_sem.at[0])
    arrived(gp_send.at[pl.ds(0, 12)], gp_send_sem)
    arrived(out_a, st2_send.at[0])
    arrived(out_b, st2_send.at[1])
    arrived(gq_send.at[pl.ds(0, NZ - 1)], gq_sem.at[0])
    arrived(loss_x.at[pl.ds(0, 3)], loss_sem.at[0])
    arrived(loss_y.at[pl.ds(0, 3)], loss_sem.at[2])
    phase(None)


def write_out(gq_in, gp_in, loss_in, gq_hbm, gp_hbm, loss_out, sem):
    copies = [
        pltpu.make_async_copy(gp_in, gp_hbm, sem.at[0]),
        pltpu.make_async_copy(gq_in, gq_hbm, sem.at[1]),
    ]
    for copy in copies:
        copy.start()
    loss_out[0] = loss_in[0, 0]
    for copy in copies:
        copy.wait()


def on_device(queries, query_mask, positive, page_vectors, page_mask):
    hbm = pl.BlockSpec(memory_space=pl.ANY)
    vmem = pl.BlockSpec(memory_space=pltpu.VMEM)
    smem = pl.BlockSpec(memory_space=pltpu.SMEM)
    V = pltpu.VMEM
    dma = pltpu.SemaphoreType.DMA
    scratch = [
        pltpu.SMEM((1, TOK), I32),
        pltpu.SMEM((1, 1), I32),
        V((2, 128, D), BF16),
        V((2, 128), I32),
        dma((5,)),
        V((2, NZ, TOK + 8, D), BF16),
        V((NS, 2, 128, D), BF16),
        V((D, NS * 256), BF16),
        V((2, D, ROWS), BF16),
        V((NS * 256, 2 * ROWS), BF16),
        V((2, NS, 2, 128, ROWS), F32),
        V((2, 32, ROWS), F32),
        V((2, 32, ROWS), F32),
        V((32, 128), F32),
        V((2, 32, ROWS), F32),
        V((2, 32, ROWS), F32),
        V((32, 1, 128), F32),
        V((2, D, ROWS), F32),
        V((NS, 2, 128, D), BF16),
        V((4, 128, D), F32),
        V((4, 128, D), F32),
        V((4, 3, 128, D), BF16),
        V((4, 3, 128, D), BF16),
        V((3, 128, D), BF16),
        V((3, 128, D), BF16),
        V((3, 128, D), BF16),
        V((3, 128, D), BF16),
        V((ROWS, D), F32),
        V((ROWS, D), F32),
        V((ROWS, D), F32),
        V((NZ, TOK, D), BF16),
        V((NZ, TOK, D), BF16),
        V((4, 1, 128), F32),
        V((4, 1, 128), F32),
        dma(()),
        dma((3,)),
        dma((2,)),
        dma((2,)),
        dma(()),
        dma((2, 3)),
        dma((4,)),
        dma((2,)),
        dma(()),
        dma((2, 4)),
        dma((2,)),
        dma((2,)),
        dma((2,)),
        dma((4,)),
    ]
    partial = pl.pallas_call(
        kernel,
        out_shape=(V((1, TOK, D), F32), V((2, 128, D), F32), V((1, 128), F32)),
        in_specs=[hbm] * 5,
        out_specs=(vmem, vmem, vmem),
        scratch_shapes=scratch,
        compiler_params=pltpu.CompilerParams(collective_id=0, has_side_effects=True),
    )(queries, query_mask, positive.reshape(1, 1), page_vectors, page_mask)
    gq, gp, loss = pl.pallas_call(
        write_out,
        out_shape=(
            jax.ShapeDtypeStruct((1, TOK, D), F32),
            jax.ShapeDtypeStruct((2, 128, D), F32),
            jax.ShapeDtypeStruct((1,), F32),
        ),
        in_specs=[vmem] * 3,
        out_specs=(hbm, hbm, smem),
        scratch_shapes=[dma((2,))],
        compiler_params=pltpu.CompilerParams(vmem_limit_bytes=1 << 20),
    )(*[pltpu.with_memory_space_constraint(p, pltpu.VMEM) for p in partial])
    return gq, gp, loss.reshape(())


def solution(mesh):
    split = Mesh(mesh.devices.reshape(2, 4, 2, 2, 16), AXES)
    return jax.shard_map(
        on_device,
        mesh=split,
        in_specs=(P(AXES, None, None), P(AXES, None), P(AXES), P(AXES, None, None), P(AXES, None)),
        out_specs=(P(AXES, None, None), P(AXES, None, None), P()),
        check_vma=False,
    )
```

time: 51.9 us -> 47.9 us (0.923)
  Pallas kernels: 50.5 us -> 46.4 us
    pallas_call x1, Pallas kernels: 49.3 us -> 45.2 us  [on_device(): pl.pallas_call(kernel, out_shape=(V((1, TOK, D), F32), V((2, 128, D), F32...]
where the time goes in v3:
time: 47.9 us; the launch traced here: 47.7 us
  Pallas kernels  46.4 us (97%)
  between operations  1.28 us (3%)
    pallas_call x1, Pallas kernels, on_device(): pl.pallas_call(kernel, out_shape=(V((1, TOK, D), F32), V((2, 128, D), F32...  45.2 us
    pallas_call x1, Pallas kernels, on_device(): pl.pallas_call(write_out, out_shape=(jax.ShapeDtypeStruct((1, TOK, D), F3...  1.19 us

profile of v3, /device:TPU:1, one launch (start us, length us, event | category | flops | bytes accessed | tf_op | source)
XLA Modules:
  0.0 47.7 jit_solution(9355816613317644689)
XLA Ops:
  1.3 45.2 %shard_map.76 = (f32[1,16,128]{2,1,0:T(8,128)S(1)}, f32[2,128,128]{2,1,0:T(8,128)S(1)}, f32[1,128]{1,0:T(1,128)S(1)}) custom-call(bf16[1,16,128]{2,1,0:T(8,128)(2,1)} %q_hbm.1, s32[1,16]{1,0:T(1,128)} %qmask_hbm.1, s32[1,1]{1,0:T(1,128)} %bitcast.2.pos_hbm, bf16[2,128,128]{2,1,0:T(8,128)(2,1)} %pg_hbm.1, s32[2,128]{1,0:T(2,128)} %pmask_hbm.1), custom_call_target="tpu_custom_call" | custom-call | tf_op jit(solution)/shard_map/pallas_call | solution.py:497
  46.5 1.2 %shard_map.77 = (f32[1,16,128]{2,1,0:T(8,128)}, f32[2,128,128]{2,1,0:T(8,128)}, f32[1]{0:T(128)}) custom-call(f32[1,16,128]{2,1,0:T(8,128)S(1)} %get-tuple-element.9.gq_in, f32[2,128,128]{2,1,0:T(8,128)S(1)} %get-tuple-element.10.gp_in, f32[1,128]{1,0:T(1,128)S(1)} %get-tuple-element.11.loss_in), custom_call_target="tpu_custom_call" | custom-call | tf_op jit(solution)/shard_map/pallas_call | solution.py:505

commit v4 on v3

--- a/solution.py
+++ b/solution.py
@@ -1,3 +1,5 @@
+import math
+
 import jax
 import jax.numpy as jnp
 from jax import lax
@@ -16,6 +18,7 @@
 ROWS = NZ * TOK
 STEP = 4
 FLOOR = -1e30
+RATE = 2.0 * math.log2(math.e)
 MARK = 128.0
 
 
@@ -23,8 +26,14 @@
     return lax.broadcasted_iota(I32, shape, dim)
 
 
-def exact_dot(a, b):
-    return jnp.dot(a, b, preferred_element_type=F32, precision=lax.Precision.HIGHEST)
+def select_dot(a, chooser):
+    parts, rest = [], a
+    for _ in range(3):
+        parts.append(rest.astype(BF16))
+        rest = rest - parts[-1].astype(F32)
+    n = a.shape[0]
+    out = jnp.dot(jnp.concatenate(parts, axis=0), chooser, preferred_element_type=F32)
+    return out[:n] + out[n : 2 * n] + out[2 * n :]
 
 
 def kernel(
@@ -45,6 +54,9 @@
     pages,
     pages_t,
     q_t,
+    bias,
+    same,
+    spread,
     factor,
     e_all,
     top,
@@ -136,6 +148,14 @@
     ]
     for load in loads:
         load.start()
+    krow = iota((D, ROWS), 0)
+    for h in range(2):
+        q_t[h, pl.ds(D, D), :] = jnp.where(krow == 0, 1.0, 0.0).astype(BF16)
+    together = lax.shift_right_logical(iota((ROWS, ROWS), 0), 4) == lax.shift_right_logical(iota((ROWS, ROWS), 1), 4)
+    same[...] = jnp.where(together, 1.0, 0.0).astype(BF16)
+    lane_out = iota((128, 512), 1)
+    source = jnp.bitwise_and(lane_out, 112) + lax.shift_right_logical(lane_out, 7)
+    spread[...] = jnp.where(iota((128, 512), 0) == source, 1.0, 0.0).astype(BF16)
     for load in loads:
         load.wait()
     prow = iota((128, 128), 0)
@@ -149,8 +169,8 @@
     for t in range(TOK):
         mask = mask + jnp.where(lane == base + t, qmask[0, t], 0)
     group = lax.shift_right_logical(lane, 4) == lax.rem(z, 8)
-    page_hi = jnp.where(group, lax.shift_right_logical(pos[0, 0], 5), 0)
-    page_lo = jnp.where(group, jnp.bitwise_and(pos[0, 0], 31), 0)
+    page_hi = jnp.where(group, lax.shift_right_logical(pos[0], 5), 0)
+    page_lo = jnp.where(group, jnp.bitwise_and(pos[0], 31), 0)
     mrow = iota((8, 128), 0)
     meta = jnp.where(mrow == 0, mask, jnp.where(mrow == 1, page_hi, jnp.where(mrow == 2, page_lo, 0)))
     q_all[c, z, pl.ds(TOK, 8), :] = meta.astype(F32).astype(BF16)
@@ -160,8 +180,13 @@
 
     phase("issue")
 
-    def send_query(zsrc, d, i):
-        push(q_all.at[c, zsrc], q_all.at[c, zsrc], q_send, q_recv.at[i], at_z(d))
+    for d in reversed(near):
+        sem = q_recv.at[0 if d == STEP else 1 if d == NZ - STEP else 2]
+        push(q_all.at[c, z], q_all.at[c, z], q_send.at[0], sem, at_z(d))
+
+    def pass_query(zsrc, d):
+        push(q_all.at[c, zsrc], q_all.at[c, zsrc], q_send.at[0], q_recv.at[3], at_z(d))
+        push(q_all.at[c, zsrc], q_all.at[c, zsrc], q_send.at[1], q_recv.at[5], {"c": other, **at_z(d)})
 
     for d in (2, 1, 3):
         push(pages.at[0, 0], pages.at[4 * (4 - d), 0], pg_send, line_recv.at[0, d - 1], at_x(d))
@@ -170,77 +195,94 @@
         push(pages.at[0, 1], pages.at[4 * (4 - d), 1], pg_send, far_recv.at[0], at_x(d))
         push(pages.at[0, 0], pages.at[4 - d, 0], pg_send, far_recv.at[0], at_y(d))
 
-    for d in reversed(near):
-        send_query(z, d, 0 if d == STEP else 1 if d == NZ - STEP else 2)
-
-    def got_query(d, i):
-        zsrc = lax.rem(z + d, NZ)
-        arrived(q_all.at[c, zsrc], q_recv.at[i])
-        return zsrc
-
-    phase("relay")
-    for d in (1, 3, 2):
+    def relay(d):
         arrived(pages.at[4 * d, 0], line_recv.at[0, 3 - d])
         for e in (2, 1, 3):
-            push(pages.at[4 * d, 0], pages.at[4 * d + 4 - e, 0], pg_send, far_recv.at[d], at_y(e))
+            push(pages.at[4 * d, 0], pages.at[4 * d + 4 - e, 0], pg_send, far_recv.at[1], at_y(e))
         arrived(pages.at[d, 1], line_recv.at[1, 3 - d])
         for e in (2, 1, 3):
-            push(pages.at[d, 1], pages.at[4 * (4 - e) + d, 1], pg_send, far_recv.at[4 - e], at_x(e))
-
+            push(pages.at[d, 1], pages.at[4 * (4 - e) + d, 1], pg_send, far_recv.at[1], at_x(e))
+
+    phase("relay")
+    relay(1)
+    relay(3)
     phase("query_near")
-    behind = got_query(NZ - STEP, 0)
+    arrived(q_all.at[c, pl.ds(0, 6)], q_recv.at[2])
+    behind, ahead = lax.rem(z + NZ - STEP, NZ), lax.rem(z + STEP, NZ)
+    arrived(q_all.at[c, behind], q_recv.at[0])
+    arrived(q_all.at[c, ahead], q_recv.at[1])
     for d in range(STEP, 0, -1):
-        send_query(behind, d, 2)
-    ahead = got_query(STEP, 1)
+        pass_query(behind, d)
     for d in range(STEP - 1, 0, -1):
-        send_query(ahead, NZ - d, 2)
-
-    phase("query_far")
-    arrived(q_all.at[c, pl.ds(0, 13)], q_recv.at[2])
-    push(q_all.at[c], q_all.at[c], pair_send.at[0], pair_recv.at[0], pair)
+        pass_query(ahead, NZ - d)
+    for d in [0] + near:
+        zsrc = lax.rem(z + d, NZ)
+        push(q_all.at[c, zsrc], q_all.at[c, zsrc], q_send.at[1], q_recv.at[4], pair)
+    phase("relay_2")
+    relay(2)
 
     def turn_queries(h):
-        q_t[h] = (q_all[h, :, pl.ds(0, TOK), :].reshape(ROWS, D).astype(F32) * 2.0).T.astype(BF16)
-
-    def forward(h, slots):
+        q_t[h, pl.ds(0, D), :] = q_all[h, :, pl.ds(0, TOK), :].reshape(ROWS, D).T
+
+    first = iota((128, 128), 1) == 0
+
+    def count_patches(slots):
         for rx, ry in slots:
             s = 4 * rx + ry
             for k in range(2):
                 last = pages[s, k, pl.ds(112, 16), :].astype(F32)[15:16]
                 count = jnp.where(last > 100.0, last - MARK, 128.0)
-                live = prow < jnp.broadcast_to(count.astype(I32), (128, 128))
+                logn[pl.ds(2 * s + k, 1), :] = count
+                unused = jnp.logical_and(first, prow >= jnp.broadcast_to(count.astype(I32), (128, 128)))
+                bias[s, pl.ds(128 * k, 128), :] = jnp.where(unused, FLOOR, 0.0).astype(BF16)
+
+    def forward(h, slots):
+        for rx, ry in slots:
+            s = 4 * rx + ry
+            block = jnp.concatenate([pages[s].reshape(256, D), bias[s]], axis=1)
+            dots = jnp.dot(block, q_t[h], preferred_element_type=F32)
+            for k in range(2):
                 row = pl.ds(2 * s + k, 1)
-                logn[row, :] = count
-                logits = jnp.dot(pages[s, k], q_t[h], preferred_element_type=F32)
                 for v in range(2):
                     lanes = pl.ds(128 * v, 128)
-                    part = jnp.where(live, logits[:, 128 * v : 128 * v + 128], FLOOR)
+                    part = dots[128 * k : 128 * k + 128, 128 * v : 128 * v + 128]
                     highest = jnp.max(part, axis=0, keepdims=True)
-                    e = jnp.exp(part - highest)
+                    e = jnp.exp2((part - highest) * RATE)
                     e_all[h, s, k, :, lanes] = e
-                    top[h, row, lanes] = highest
+                    top[h, row, lanes] = highest * 2.0
                     tot[h, row, lanes] = jnp.sum(e, axis=0, keepdims=True)
 
     line_slots = [(0, 0), (1, 0), (0, 1), (3, 0), (0, 3), (2, 0), (0, 2)]
     far_slots = [(dx, dy) for dx in (1, 3, 2) for dy in (1, 3, 2)]
-    phase("forward_own")
-    turn_queries(c)
     arrived(pages.at[pl.ds(0, 3)], far_recv.at[0])
-    forward(c, line_slots)
+    count_patches(line_slots)
+    def own_far():
+        arrived(q_all.at[c, pl.ds(0, 7)], q_recv.at[3])
+
+    def other_core():
+        arrived(q_all.at[other, pl.ds(0, 9)], q_recv.at[4])
+        arrived(q_all.at[other, pl.ds(0, 7)], q_recv.at[5])
+
+    phase("query_far")
+    pl.when(c == 1)(own_far)
+    pl.when(c == 0)(other_core)
+    phase("forward_1")
+    turn_queries(1)
+    forward(1, line_slots)
+    phase("query_pair")
+    pl.when(c == 0)(own_far)
+    pl.when(c == 1)(other_core)
+    phase("forward_0")
+    turn_queries(0)
+    forward(0, line_slots)
     phase("pages_far")
-    for dx in (1, 2, 3):
-        arrived(pages.at[pl.ds(4 * dx + 1, 3)], far_recv.at[dx])
+    arrived(pages.at[pl.ds(0, 9)], far_recv.at[1])
     phase("forward_far")
-    forward(c, far_slots)
-    phase("query_pair")
-    arrived(q_all.at[other], pair_recv.at[0])
-    phase("forward_other")
-    turn_queries(other)
-    forward(other, line_slots + far_slots)
+    count_patches(far_slots)
+    forward(1, far_slots)
+    forward(0, far_slots)
 
     phase("scores")
-    same = lax.shift_right_logical(iota((ROWS, ROWS), 0), 4) == lax.shift_right_logical(iota((ROWS, ROWS), 1), 4)
-    same = jnp.where(same, 1.0, 0.0).astype(F32)
     i = iota((32, ROWS), 0)
     px = jnp.bitwise_and(x + lax.shift_right_logical(i, 3), 3)
     py = jnp.bitwise_and(y + jnp.bitwise_and(lax.shift_right_logical(i, 1), 3), 3)
@@ -257,7 +299,7 @@
         chosen.append(page_id.astype(F32) == both[1:2] * 32.0 + both[2:3])
         lse = top[h] + jnp.log(tot[h])
         value = masks[h] * (0.5 * (lse - log_count))
-        total = exact_dot(value, same)
+        total = select_dot(value, same[...])
         score[h] = total
         highest = jnp.max(total, axis=0, keepdims=True)
         lse_rows.append(highest + jnp.log(jnp.sum(jnp.exp(total - highest), axis=0, keepdims=True)))
@@ -300,12 +342,7 @@
     loss_x[x] = column_loss
     for d in (1, 2, 3):
         push(loss_x.at[x], loss_x.at[x], loss_sem.at[0], loss_sem.at[1], at_x(d))
-    lane_in, lane_out = iota((128, 512), 0), iota((128, 512), 1)
-    source = lax.shift_left(lax.shift_right_logical(jnp.bitwise_and(lane_out, 127), 4), 4) + lax.shift_right_logical(
-        lane_out, 7
-    )
-    spread = jnp.where(lane_in == source, 1.0, 0.0).astype(F32)
-    wide = exact_dot(jnp.broadcast_to(page_lse, (8, 128)), spread)[0:1]
+    wide = select_dot(jnp.broadcast_to(page_lse, (8, 128)), spread[...])[0:1]
     for h in range(2):
         coefficient = jnp.exp(score[h] - wide[:, 256 * h : 256 * h + 256]) - jnp.where(chosen[h], 1.0, 0.0)
         coef[h] = coefficient * masks[h] / tot[h]
@@ -319,45 +356,72 @@
             value = e_all[h, s, k] * coef[h, pl.ds(2 * s + k, 1), :]
             factor[pl.ds(128 * i, 128), pl.ds(ROWS * h, ROWS)] = value.astype(BF16)
 
-    def page_grads(start, size):
-        grads = jnp.dot(factor[pl.ds(128 * start, 128 * size), :], queries, preferred_element_type=F32)
-        for i in range(size):
-            s, k = order[start + i]
+    def page_grads(start, stop):
+        size = 2 if stop - start == 4 else 4
+        for part in range(start, stop, size):
+            grads = jnp.dot(factor[pl.ds(128 * part, 128 * size), :], queries, preferred_element_type=F32)
+            for i in range(size):
+                s, k = order[part + i]
+                rx, ry = s // 4, s % 4
+                g = grads[128 * i : 128 * i + 128]
+                if (rx if k else ry) == 0:
+                    (own_b if k else own_a)[ry if k else rx] = g
+                else:
+                    gp_send[s, k] = g.astype(BF16)
+        for s, k in order[start:stop]:
             rx, ry = s // 4, s % 4
-            g = grads[128 * i : 128 * i + 128]
             if k == 0 and ry:
-                gp_send[s, 0] = g.astype(BF16)
                 push(gp_send.at[s, 0], mid_a.at[rx, 3 - ry], gp_send_sem, gp_recv.at[0, rx], at_y(ry))
-            elif k == 0:
-                own_a[rx] = g
-            elif rx:
-                gp_send[s, 1] = g.astype(BF16)
+            elif k == 1 and rx:
                 push(gp_send.at[s, 1], mid_b.at[ry, 3 - rx], gp_send_sem, gp_recv.at[1, ry], at_x(rx))
-            else:
-                own_b[ry] = g
 
     def query_grads():
         for h in range(2):
             gq_t[h] = jnp.dot(pages_t[...], factor[:, pl.ds(ROWS * h, ROWS)], preferred_element_type=F32)
         gq_pair[...] = gq_t[other].T
-        push(gq_pair, gq_in, pair_send.at[1], pair_recv.at[1], pair)
+        push(gq_pair, gq_in, pair_send, pair_recv, pair)
         gq_own[...] = gq_t[c].T
 
     def query_grads_away():
-        arrived(gq_in, pair_recv.at[1])
+        arrived(gq_in, pair_recv)
         gq_own[...] += gq_in[...]
         gq_send[...] = gq_own[...].astype(BF16).reshape(NZ, TOK, D)
         for d in (8, 7, 9, 6, 10, 5, 11, 4, 12, 3, 13, 2, 14, 1, 15):
             zz = lax.rem(z + d, NZ)
             push(gq_send.at[zz], gq_recv.at[z], gq_sem.at[0], gq_sem.at[1], at_z(d))
 
+    def line_sum(r):
+        arrived(mid_a.at[r], gp_recv.at[0, r])
+        acc_a = own_a[r] + (mid_a[r, 0].astype(F32) + mid_a[r, 1].astype(F32) + mid_a[r, 2].astype(F32))
+        if r:
+            out_a[r - 1] = acc_a.astype(BF16)
+            push(out_a.at[r - 1], in_a.at[3 - r], st2_send.at[0], st2_recv.at[0], at_x(r))
+        else:
+            own_a[0] = acc_a
+        arrived(mid_b.at[r], gp_recv.at[1, r])
+        acc_b = own_b[r] + (mid_b[r, 0].astype(F32) + mid_b[r, 1].astype(F32) + mid_b[r, 2].astype(F32))
+        if r:
+            out_b[r - 1] = acc_b.astype(BF16)
+            push(out_b.at[r - 1], in_b.at[3 - r], st2_send.at[1], st2_recv.at[1], at_y(r))
+        else:
+            own_b[0] = acc_b
+
+    def pass_loss():
+        arrived(loss_x.at[pl.ds(0, 3)], loss_sem.at[1])
+        line = loss_x[0] + loss_x[1] + loss_x[2] + loss_x[3]
+        loss_y[y] = line
+        for d in (1, 2, 3):
+            push(loss_y.at[y], loss_y.at[y], loss_sem.at[2], loss_sem.at[3], at_y(d))
+
     @pl.when(z < 4)
     def _():
-        for start in range(0, 32, 4):
-            for i in range(4):
-                form_factor(start + i)
-            page_grads(start, 4)
+        for start, stop in ((0, 4), (4, 8), (8, 16), (16, 24), (24, 32)):
+            for i in range(start, stop):
+                form_factor(i)
+            page_grads(start, stop)
         query_grads()
+        pass_loss()
+        line_sum(2)
         query_grads_away()
 
     @pl.when(z >= 4)
@@ -365,33 +429,19 @@
         for i in range(32):
             form_factor(i)
         query_grads()
-        for start in range(0, 16, 4):
-            page_grads(start, 4)
+        page_grads(0, 8)
+        page_grads(8, 16)
         query_grads_away()
-        for start in range(16, 32, 4):
-            page_grads(start, 4)
-
-    phase("loss_line")
-    arrived(loss_x.at[pl.ds(0, 3)], loss_sem.at[1])
-    line = loss_x[0] + loss_x[1] + loss_x[2] + loss_x[3]
-    loss_y[y] = line
-    for d in (1, 2, 3):
-        push(loss_y.at[y], loss_y.at[y], loss_sem.at[2], loss_sem.at[3], at_y(d))
+        page_grads(16, 24)
+        page_grads(24, 32)
+        pass_loss()
+        line_sum(2)
 
     phase("lines")
-    for r in (2, 1, 3, 0):
-        arrived(mid_a.at[r], gp_recv.at[0, r])
-        acc_a = own_a[r] + (mid_a[r, 0].astype(F32) + mid_a[r, 1].astype(F32) + mid_a[r, 2].astype(F32))
-        arrived(mid_b.at[r], gp_recv.at[1, r])
-        acc_b = own_b[r] + (mid_b[r, 0].astype(F32) + mid_b[r, 1].astype(F32) + mid_b[r, 2].astype(F32))
-        if r:
-            out_a[r - 1] = acc_a.astype(BF16)
-            push(out_a.at[r - 1], in_a.at[3 - r], st2_send.at[0], st2_recv.at[0], at_x(r))
-            out_b[r - 1] = acc_b.astype(BF16)
-            push(out_b.at[r - 1], in_b.at[3 - r], st2_send.at[1], st2_recv.at[1], at_y(r))
-        else:
-            own_a[0] = acc_a
-            own_b[0] = acc_b
+    line_sum(1)
+    line_sum(3)
+    phase("line_own")
+    line_sum(0)
 
     phase("loss")
     arrived(loss_y.at[pl.ds(0, 3)], loss_sem.at[3])
@@ -412,10 +462,10 @@
     gq_ref[0] = total
 
     phase("drain")
-    arrived(q_all.at[c, pl.ds(0, NZ - 1)], q_send)
+    arrived(q_all.at[c, pl.ds(0, NZ - 1)], q_send.at[0])
+    arrived(q_all.at[c], q_send.at[1])
     arrived(pages.at[pl.ds(0, NS - 1)], pg_send)
-    arrived(q_all.at[c], pair_send.at[0])
-    arrived(gq_pair, pair_send.at[1])
+    arrived(gq_pair, pair_send)
     arrived(stat.at[pl.ds(0, 31)], stat_sem.at[0])
     arrived(gp_send.at[pl.ds(0, 12)], gp_send_sem)
     arrived(out_a, st2_send.at[0])
@@ -446,14 +496,17 @@
     dma = pltpu.SemaphoreType.DMA
     scratch = [
         pltpu.SMEM((1, TOK), I32),
-        pltpu.SMEM((1, 1), I32),
+        pltpu.SMEM((1,), I32),
         V((2, 128, D), BF16),
         V((2, 128), I32),
         dma((5,)),
         V((2, NZ, TOK + 8, D), BF16),
         V((NS, 2, 128, D), BF16),
         V((D, NS * 256), BF16),
-        V((2, D, ROWS), BF16),
+        V((2, 2 * D, ROWS), BF16),
+        V((NS, 256, 128), BF16),
+        V((ROWS, ROWS), BF16),
+        V((128, 512), BF16),
         V((NS * 256, 2 * ROWS), BF16),
         V((2, NS, 2, 128, ROWS), F32),
         V((2, 32, ROWS), F32),
@@ -479,13 +532,13 @@
         V((NZ, TOK, D), BF16),
         V((4, 1, 128), F32),
         V((4, 1, 128), F32),
+        dma((2,)),
+        dma((6,)),
         dma(()),
-        dma((3,)),
-        dma((2,)),
-        dma((2,)),
+        dma(()),
         dma(()),
         dma((2, 3)),
-        dma((4,)),
+        dma((2,)),
         dma((2,)),
         dma(()),
         dma((2, 4)),
@@ -497,11 +550,11 @@
     partial = pl.pallas_call(
         kernel,
         out_shape=(V((1, TOK, D), F32), V((2, 128, D), F32), V((1, 128), F32)),
-        in_specs=[hbm] * 5,
+        in_specs=[hbm, hbm, pl.BlockSpec(memory_space=pltpu.HBM), hbm, hbm],
         out_specs=(vmem, vmem, vmem),
         scratch_shapes=scratch,
         compiler_params=pltpu.CompilerParams(collective_id=0, has_side_effects=True),
-    )(queries, query_mask, positive.reshape(1, 1), page_vectors, page_mask)
+    )(queries, query_mask, positive, page_vectors, page_mask)
     gq, gp, loss = pl.pallas_call(
         write_out,
         out_shape=(

time: 47.9 us -> 46.5 us (0.971)
  Pallas kernels: 46.4 us -> 45 us
    pallas_call x1, Pallas kernels: 45.2 us -> 43.8 us  [on_device(): pl.pallas_call(kernel, out_shape=(V((1, TOK, D), F32), V((2, 128, D), F32...]
where the time goes in v4:
time: 46.5 us; the launch traced here: 46.3 us
  Pallas kernels  45 us (97%)
  between operations  1.28 us (3%)
    pallas_call x1, Pallas kernels, on_device(): pl.pallas_call(kernel, out_shape=(V((1, TOK, D), F32), V((2, 128, D), F32...  43.8 us
    pallas_call x1, Pallas kernels, on_device(): pl.pallas_call(write_out, out_shape=(jax.ShapeDtypeStruct((1, TOK, D), F3...  1.19 us

profile of v4, /device:TPU:1, one launch (start us, length us, event | category | flops | bytes accessed | tf_op | source)
XLA Modules:
  0.0 46.3 jit_solution(12171303235892690778)
XLA Ops:
  1.3 43.8 %shard_map.76 = (f32[1,16,128]{2,1,0:T(8,128)S(1)}, f32[2,128,128]{2,1,0:T(8,128)S(1)}, f32[1,128]{1,0:T(1,128)S(1)}) custom-call(bf16[1,16,128]{2,1,0:T(8,128)(2,1)} %q_hbm.1, s32[1,16]{1,0:T(1,128)} %qmask_hbm.1, s32[1]{0:T(128)S(6)} %copy.8.pos_hbm, bf16[2,128,128]{2,1,0:T(8,128)(2,1)} %pg_hbm.1, s32[2,128]{1,0:T(2,128)} %pmask_hbm.1), custom_call_target="tpu_custom_call" | custom-call | tf_op jit(solution)/shard_map/pallas_call | solution.py:550
  45.1 1.2 %shard_map.77 = (f32[1,16,128]{2,1,0:T(8,128)}, f32[2,128,128]{2,1,0:T(8,128)}, f32[1]{0:T(128)}) custom-call(f32[1,16,128]{2,1,0:T(8,128)S(1)} %get-tuple-element.9.gq_in, f32[2,128,128]{2,1,0:T(8,128)S(1)} %get-tuple-element.10.gp_in, f32[1,128]{1,0:T(1,128)S(1)} %get-tuple-element.11.loss_in), custom_call_target="tpu_custom_call" | custom-call | tf_op jit(solution)/shard_map/pallas_call | solution.py:558

commit v5 on v4

--- a/solution.py
+++ b/solution.py
@@ -269,18 +269,17 @@
     phase("forward_1")
     turn_queries(1)
     forward(1, line_slots)
+    phase("pages_far")
+    arrived(pages.at[pl.ds(0, 9)], far_recv.at[1])
+    phase("forward_far")
+    count_patches(far_slots)
+    forward(1, far_slots)
     phase("query_pair")
     pl.when(c == 0)(own_far)
     pl.when(c == 1)(other_core)
     phase("forward_0")
     turn_queries(0)
-    forward(0, line_slots)
-    phase("pages_far")
-    arrived(pages.at[pl.ds(0, 9)], far_recv.at[1])
-    phase("forward_far")
-    count_patches(far_slots)
-    forward(1, far_slots)
-    forward(0, far_slots)
+    forward(0, line_slots + far_slots)
 
     phase("scores")
     i = iota((32, ROWS), 0)
@@ -476,14 +475,15 @@
     phase(None)
 
 
-def write_out(gq_in, gp_in, loss_in, gq_hbm, gp_hbm, loss_out, sem):
+def write_out(gq_in, gp_in, loss_in, gq_hbm, gp_hbm, loss_hbm, loss_out, sem):
+    loss_out[0] = loss_in[0, 0]
     copies = [
         pltpu.make_async_copy(gp_in, gp_hbm, sem.at[0]),
         pltpu.make_async_copy(gq_in, gq_hbm, sem.at[1]),
+        pltpu.make_async_copy(loss_out, loss_hbm, sem.at[2]),
     ]
     for copy in copies:
         copy.start()
-    loss_out[0] = loss_in[0, 0]
     for copy in copies:
         copy.wait()
 
@@ -491,7 +491,6 @@
 def on_device(queries, query_mask, positive, page_vectors, page_mask):
     hbm = pl.BlockSpec(memory_space=pl.ANY)
     vmem = pl.BlockSpec(memory_space=pltpu.VMEM)
-    smem = pl.BlockSpec(memory_space=pltpu.SMEM)
     V = pltpu.VMEM
     dma = pltpu.SemaphoreType.DMA
     scratch = [
@@ -563,8 +562,8 @@
             jax.ShapeDtypeStruct((1,), F32),
         ),
         in_specs=[vmem] * 3,
-        out_specs=(hbm, hbm, smem),
-        scratch_shapes=[dma((2,))],
+        out_specs=(hbm, hbm, pl.BlockSpec(memory_space=pltpu.HBM)),
+        scratch_shapes=[pltpu.SMEM((1,), F32), dma((3,))],
         compiler_params=pltpu.CompilerParams(vmem_limit_bytes=1 << 20),
     )(*[pltpu.with_memory_space_constraint(p, pltpu.VMEM) for p in partial])
     return gq, gp, loss.reshape(())

time: 46.5 us -> 45.8 us (0.985)
  Pallas kernels: 45 us -> 44.1 us
    pallas_call x1, Pallas kernels: 1.19 us -> 0.69 us  [on_device(): pl.pallas_call(write_out, out_shape=(jax.ShapeDtypeStruct((1, TOK, D), F3...]
where the time goes in v5:
time: 45.8 us; the launch traced here: 45.4 us
  Pallas kernels  44.1 us (96%)
  between operations  1.28 us (3%)
    pallas_call x1, Pallas kernels, on_device(): pl.pallas_call(kernel, out_shape=(V((1, TOK, D), F32), V((2, 128, D), F32...  43.4 us

profile of v5, /device:TPU:1, one launch (start us, length us, event | category | flops | bytes accessed | tf_op | source)
XLA Modules:
  0.0 45.4 jit_solution(5950464663388039423)
XLA Ops:
  1.3 43.4 %shard_map.76 = (f32[1,16,128]{2,1,0:T(8,128)S(1)}, f32[2,128,128]{2,1,0:T(8,128)S(1)}, f32[1,128]{1,0:T(1,128)S(1)}) custom-call(bf16[1,16,128]{2,1,0:T(8,128)(2,1)} %q_hbm.1, s32[1,16]{1,0:T(1,128)} %qmask_hbm.1, s32[1]{0:T(128)S(6)} %copy.8.pos_hbm, bf16[2,128,128]{2,1,0:T(8,128)(2,1)} %pg_hbm.1, s32[2,128]{1,0:T(2,128)} %pmask_hbm.1), custom_call_target="tpu_custom_call" | custom-call | tf_op jit(solution)/shard_map/pallas_call | solution.py:549
  44.7 0.7 %shard_map.77 = (f32[1,16,128]{2,1,0:T(8,128)}, f32[2,128,128]{2,1,0:T(8,128)}, f32[1]{0:T(128)}) custom-call(f32[1,16,128]{2,1,0:T(8,128)S(1)} %get-tuple-element.9.gq_in, f32[2,128,128]{2,1,0:T(8,128)S(1)} %get-tuple-element.10.gp_in, f32[1,128]{1,0:T(1,128)S(1)} %get-tuple-element.11.loss_in), custom_call_target="tpu_custom_call" | custom-call | tf_op jit(solution)/shard_map/pallas_call | solution.py:557

commit v6 on v5

--- a/solution.py
+++ b/solution.py
@@ -290,6 +290,7 @@
     log_count = jnp.log(logn[...])
     log_count = jnp.concatenate([log_count, log_count], axis=1)
     masks, chosen, lse_rows, picked_rows = [], [], [], []
+    values = []
     for h in range(2):
         lo = sum(q_all[h, t, pl.ds(TOK, 8), :].astype(F32) for t in range(8))
         hi = sum(q_all[h, t, pl.ds(TOK, 8), :].astype(F32) for t in range(8, 16))
@@ -297,8 +298,10 @@
         masks.append(both[0:1])
         chosen.append(page_id.astype(F32) == both[1:2] * 32.0 + both[2:3])
         lse = top[h] + jnp.log(tot[h])
-        value = masks[h] * (0.5 * (lse - log_count))
-        total = select_dot(value, same[...])
+        values.append(masks[h] * (0.5 * (lse - log_count)))
+    totals = select_dot(jnp.concatenate(values, axis=0), same[...])
+    for h in range(2):
+        total = totals[32 * h : 32 * h + 32]
         score[h] = total
         highest = jnp.max(total, axis=0, keepdims=True)
         lse_rows.append(highest + jnp.log(jnp.sum(jnp.exp(total - highest), axis=0, keepdims=True)))

time: 45.8 us -> 45.9 us (level)
  no operation moved by 1% of the time
where the time goes in v6:
time: 45.9 us; the launch traced here: 45.5 us
  Pallas kernels  44.2 us (96%)
  between operations  1.28 us (3%)
    pallas_call x1, Pallas kernels, on_device(): pl.pallas_call(kernel, out_shape=(V((1, TOK, D), F32), V((2, 128, D), F32...  43.5 us

profile of v6, /device:TPU:1, one launch (start us, length us, event | category | flops | bytes accessed | tf_op | source)
XLA Modules:
  0.0 45.5 jit_solution(8699868212877020489)
XLA Ops:
  1.3 43.5 %shard_map.76 = (f32[1,16,128]{2,1,0:T(8,128)S(1)}, f32[2,128,128]{2,1,0:T(8,128)S(1)}, f32[1,128]{1,0:T(1,128)S(1)}) custom-call(bf16[1,16,128]{2,1,0:T(8,128)(2,1)} %q_hbm.1, s32[1,16]{1,0:T(1,128)} %qmask_hbm.1, s32[1]{0:T(128)S(6)} %copy.8.pos_hbm, bf16[2,128,128]{2,1,0:T(8,128)(2,1)} %pg_hbm.1, s32[2,128]{1,0:T(2,128)} %pmask_hbm.1), custom_call_target="tpu_custom_call" | custom-call | tf_op jit(solution)/shard_map/pallas_call | solution.py:552
  44.8 0.7 %shard_map.77 = (f32[1,16,128]{2,1,0:T(8,128)}, f32[2,128,128]{2,1,0:T(8,128)}, f32[1]{0:T(128)}) custom-call(f32[1,16,128]{2,1,0:T(8,128)S(1)} %get-tuple-element.9.gq_in, f32[2,128,128]{2,1,0:T(8,128)S(1)} %get-tuple-element.10.gp_in, f32[1,128]{1,0:T(1,128)S(1)} %get-tuple-element.11.loss_in), custom_call_target="tpu_custom_call" | custom-call | tf_op jit(solution)/shard_map/pallas_call | solution.py:560
